TPU v7x, 32 devices: a whole 2x2x4 slice. The times are simulated.
32 devices in a mesh: samp: 8 (over y, x, core), par: 4 (over z).
Axes of the slice: x: 2, y: 2, z: 4, core: 2. Of those that a mesh axis runs over, the one named last changes fastest.
Arguments:
- log_derivs: bfloat16 [512, 262144], P('samp', 'par')
- energies: float32 [512, 8], P('samp'), may hold values from -6 to 6
- nys_rows: int32 [8, 8], P('samp'), may hold values from 0 to 63, as said below
Outputs:
- update: float32 [262144, 8], P('par')
- solution: float32 [512, 8], P('samp')
Inputs may be any that keep to these rules, and one draw needn't show every extreme that they name: `nys_rows`: each row holds 8 different local sample numbers of that group.
All inputs are finite; a program needn't handle non-finite values.
Results may differ from a plain program's by a relative error of at most 0.014.
Values may be sent and summed in bfloat16 or wider, within the bound.
A program may use at most 128 MiB of HBM per device.

v0:
```python
import functools
import math

import jax
import jax.numpy as jnp
from jax import lax
from jax.experimental import pallas as pl
from jax.experimental.pallas import tpu as pltpu
from jax.sharding import PartitionSpec as P

ITERS = 2


damping = 0.5

MESH = pl.DeviceIdType.MESH


def factor_solve(factor, right):
    middle = lax.linalg.triangular_solve(factor, right, left_side=True, lower=True)
    return lax.linalg.triangular_solve(factor, middle, left_side=True, lower=True, transpose_a=True)


def eliminate_kernel(matrix_ref, right_ref, out_ref):
    left, right = matrix_ref[...], right_ref[...]
    row = lax.broadcasted_iota(jnp.int32, left.shape, 0)
    for i in range(left.shape[0]):
        column = left[:, i:i + 1]
        pivot = left[i:i + 1, i:i + 1]
        left_row = left[i:i + 1, :] / pivot
        right_row = right[i:i + 1, :] / pivot
        left = jnp.where(row == i, left_row, left - column * left_row)
        right = jnp.where(row == i, right_row, right - column * right_row)
    out_ref[...] = right


def small_solve(matrix, right):
    matrix = 0.5 * (matrix + matrix.T)
    return pl.pallas_call(
        eliminate_kernel, out_shape=jax.ShapeDtypeStruct(right.shape, right.dtype)
    )(matrix, right)


def hdot(left, right):
    return jnp.dot(left, right, precision=lax.Precision.HIGHEST)


def greet(peers):
    barrier = pltpu.get_barrier_semaphore()
    for peer in peers:
        pl.semaphore_signal(barrier, inc=1, device_id=peer, device_id_type=MESH)
    pl.semaphore_wait(barrier, len(peers))


def remote(src, dst, send, recv, peer):
    return pltpu.make_async_remote_copy(
        src_ref=src, dst_ref=dst, send_sem=send, recv_sem=recv, device_id=peer, device_id_type=MESH
    )


def gather_kernel(n, total_rows, scale, sums_ref, aux_ref, chosen_ref, full_ref, sketch_ref, aux_out, centered_out,
                  mean_ref, rows_out, centered_ref, land, own, full, s1, r1, s2, r2, s3, r3, s4, r4, s5, r5, s6, r6, local):
    me, col = lax.axis_index("samp"), lax.axis_index("par")
    at = [lax.rem(me + k, n) for k in range(n)]
    back = [lax.rem(me + n - k, n) for k in range(n)]
    peer = [(at[k], col) for k in range(n)]
    pair = (jnp.bitwise_xor(me, 1), col)
    width = chosen_ref.shape[1]
    half = width // 2
    part = [pl.ds(0, half), pl.ds(half, half)]
    load = pltpu.make_async_copy(full_ref, full, local.at[2])
    load.start()
    greet(peer[1:])
    scatter = [remote(sums_ref.at[at[k]], land.at[k], s1.at[k], r1.at[k], peer[k]) for k in range(1, n)]
    for copy in scatter:
        copy.start()
    sent = list(scatter)
    quad = n == 8
    beside = [jnp.bitwise_xor(me, 2), jnp.bitwise_xor(me, 4)]
    if quad:
        first = [
            remote(chosen_ref.at[:, part[d]], rows_out.at[me, :, part[d]], s4.at[d], r4.at[d], (beside[d], col))
            for d in range(2)
        ]
        for copy in first:
            copy.start()
        sent += first
    auxes = [remote(aux_ref, aux_out.at[me], s2.at[k], r2.at[k], peer[k]) for k in range(1, n)]
    mine = pltpu.make_async_copy(aux_ref, aux_out.at[me], local.at[0])
    mine.start()
    keep = pltpu.make_async_copy(chosen_ref, rows_out.at[me], local.at[1])
    keep.start()
    total = sums_ref[me]
    for k in range(1, n):
        scatter[k - 1].wait_recv()
        total = total + land[k]
    own[...] = total / total_rows
    mean_ref[me] = own[...]
    spread = [remote(own, mean_ref.at[me], s3.at[k], r3.at[k], peer[k]) for k in range(1, n)]
    for copy in spread + auxes:
        copy.start()
    sent += spread + auxes
    over = [remote(chosen_ref, rows_out.at[me], s5.at[0], r5.at[0], pair)]
    over[0].start()
    if quad:
        second = [
            remote(chosen_ref.at[:, part[1 - d]], rows_out.at[me, :, part[1 - d]], s4.at[2 + d], r4.at[2 + d],
                   (beside[d], col))
            for d in range(2)
        ]
        for copy in second:
            copy.start()
        sent += second
        for d in range(2):
            view = rows_out.at[beside[d], :, part[d]]
            remote(view, view, s4.at[d], r4.at[d], pair).wait_recv()
            step = remote(view, view, s4.at[4 + d], r4.at[4 + d], (beside[1 - d], col))
            step.start()
            sent.append(step)
    else:
        far = [remote(chosen_ref, rows_out.at[me], s4.at[k], r4.at[k], peer[k]) for k in range(2, n, 2)]
        for copy in far:
            copy.start()
        sent += far
    for k in range(1, n):
        remote(own, mean_ref.at[back[k]], s3.at[k], r3.at[k], peer[k]).wait_recv()
    load.wait()
    slab = width // n
    tile = math.gcd(slab, 1024)

    @pl.loop(0, n)
    def _(j):
        @pl.loop(0, slab // tile)
        def _(t):
            inner = pl.multiple_of(t * tile, tile)
            cols = pl.ds(pl.multiple_of(j * slab + inner, tile), tile)
            mean = mean_ref[j, :, pl.ds(inner, tile)]
            centered_ref[:, cols] = ((full[:, cols].astype(jnp.float32) - mean) * scale).astype(jnp.bfloat16)

    put = pltpu.make_async_copy(centered_ref, centered_out, local.at[2])
    put.start()
    if quad:
        for d in range(2):
            view = rows_out.at[beside[d], :, part[1 - d]]
            remote(view, view, s4.at[2 + d], r4.at[2 + d], pair).wait_recv()
            block = rows_out.at[beside[d]]
            step = remote(block, block, s5.at[1 + d], r5.at[1 + d], pair)
            step.start()
            over.append(step)
        cross = jnp.bitwise_xor(me, 6)
        for d in range(2):
            view = rows_out.at[cross, :, part[d]]
            remote(view, view, s4.at[4 + d], r4.at[4 + d], pair).wait_recv()
            step = remote(view, view, s5.at[3 + d], r5.at[3 + d], pair)
            step.start()
            over.append(step)
        block = rows_out.at[jnp.bitwise_xor(me, 1)]
        remote(block, block, s5.at[0], r5.at[0], pair).wait_recv()
        for d in range(2):
            block = rows_out.at[jnp.bitwise_xor(me, 3 + 2 * d)]
            remote(block, block, s5.at[1 + d], r5.at[1 + d], pair).wait_recv()
            view = rows_out.at[jnp.bitwise_xor(me, 7), :, part[d]]
            remote(view, view, s5.at[3 + d], r5.at[3 + d], pair).wait_recv()
    else:
        for k in range(2, n, 2):
            block = rows_out.at[back[k]]
            remote(block, block, s4.at[k], r4.at[k], pair).wait_recv()
            step = remote(block, block, s5.at[k], r5.at[k], pair)
            step.start()
            over.append(step)
        for k in range(0, n, 2):
            block = rows_out.at[lax.rem(pair[0] + n - k, n)]
            remote(block, block, s5.at[k], r5.at[k], pair).wait_recv()
    for k in range(1, n):
        remote(aux_ref, aux_out.at[back[k]], s2.at[k], r2.at[k], peer[k]).wait_recv()
    for copy in sent + over:
        copy.wait_send()
    mine.wait()
    keep.wait()
    sketch_ref[...] = jnp.zeros_like(sketch_ref)
    count = n * chosen_ref.shape[0]

    @pl.loop(0, n)
    def _(j):
        @pl.loop(0, slab // tile)
        def _(t):
            inner = pl.multiple_of(t * tile, tile)
            cols = pl.ds(pl.multiple_of(j * slab + inner, tile), tile)
            mean = mean_ref[j, :, pl.ds(inner, tile)]
            rows = rows_out[:, :, cols].astype(jnp.float32).reshape(count, tile)
            rows = ((rows - mean) * scale).astype(jnp.bfloat16)
            sketch_ref[...] += lax.dot_general(
                centered_ref[:, cols], rows, (((1,), (1,)), ((), ())), preferred_element_type=jnp.float32
            )

    put.wait()


def gather_rows(sums, aux, chosen, full, n, total_rows, scale, ident):
    dma = lambda: pltpu.SemaphoreType.DMA((n,))
    vmem = pl.BlockSpec(memory_space=pltpu.VMEM)
    slab = sums.shape[-1]
    return pl.pallas_call(
        functools.partial(gather_kernel, n, total_rows, scale),
        out_shape=(
            jax.ShapeDtypeStruct((full.shape[0], n * chosen.shape[0]), jnp.float32),
            jax.ShapeDtypeStruct((n,) + aux.shape, jnp.float32),
            jax.ShapeDtypeStruct(full.shape, full.dtype),
        ),
        in_specs=[vmem, vmem, vmem, pl.BlockSpec(memory_space=pl.ANY)],
        out_specs=(vmem, vmem, pl.BlockSpec(memory_space=pl.ANY)),
        scratch_shapes=[
            pltpu.VMEM(sums.shape, jnp.float32),
            pltpu.VMEM((n,) + chosen.shape, chosen.dtype),
            pltpu.VMEM(full.shape, full.dtype),
            pltpu.VMEM(sums.shape, jnp.float32),
            pltpu.VMEM((1, slab), jnp.float32),
            pltpu.VMEM(full.shape, full.dtype),
        ] + [dma() for _ in range(12)] + [pltpu.SemaphoreType.DMA((3,))],
        compiler_params=pltpu.CompilerParams(
            collective_id=ident, has_side_effects=True, vmem_limit_bytes=60 * 2**20
        ),
    )(sums, aux, chosen, full)


def spread_kernel(n, p, part_ref, out_ref, land, own, s1, r1, s2, r2):
    me, col = lax.axis_index("samp"), lax.axis_index("par")
    beside = [lax.rem(col + k, p) for k in range(p)]
    at = [lax.rem(me + k, n) for k in range(n)]
    back = [lax.rem(me + n - k, n) for k in range(n)]
    greet([(me, beside[k]) for k in range(1, p)] + [(at[k], col) for k in range(1, n)])
    sums = [remote(part_ref, land.at[col], s1.at[k], r1.at[k], (me, beside[k])) for k in range(1, p)]
    for copy in sums:
        copy.start()
    land[col] = part_ref[...]
    for k in range(1, p):
        there = lax.rem(col + p - k, p)
        remote(part_ref, land.at[there], s1.at[k], r1.at[k], (me, beside[k])).wait_recv()
    total = land[0]
    for j in range(1, p):
        total = total + land[j]
    own[...] = total
    out_ref[me] = total
    hops = [remote(own, out_ref.at[me], s2.at[k], r2.at[k], (at[k], col)) for k in range(1, n)]
    for copy in hops:
        copy.start()
    for k in range(1, n):
        remote(own, out_ref.at[back[k]], s2.at[k], r2.at[k], (at[k], col)).wait_recv()
    for copy in sums + hops:
        copy.wait_send()


def sum_and_spread(part, n, p, ident):
    vmem = pl.BlockSpec(memory_space=pltpu.VMEM)
    return pl.pallas_call(
        functools.partial(spread_kernel, n, p),
        out_shape=jax.ShapeDtypeStruct((n,) + part.shape, jnp.float32),
        in_specs=[vmem],
        out_specs=vmem,
        scratch_shapes=[
            pltpu.VMEM((p,) + part.shape, jnp.float32),
            pltpu.VMEM(part.shape, jnp.float32),
            pltpu.SemaphoreType.DMA((p,)),
            pltpu.SemaphoreType.DMA((p,)),
            pltpu.SemaphoreType.DMA((n,)),
            pltpu.SemaphoreType.DMA((n,)),
        ],
        compiler_params=pltpu.CompilerParams(collective_id=ident, has_side_effects=True),
    )(part)


def reduce_kernel(n, part_ref, out_ref, land, both, inbox, s0, r0, s1, r1, s2, r2, s3, r3):
    me, col = lax.axis_index("samp"), lax.axis_index("par")
    outer = n // 2
    slab = part_ref.shape[1] // n
    half = slab * outer
    i, o = lax.rem(me, 2), me // 2
    pair = (jnp.bitwise_xor(me, 1), col)
    at = [lax.rem(o + k, outer) for k in range(outer)]
    back = [lax.rem(o + outer - k, outer) for k in range(outer)]
    peer = [(at[k] * 2 + i, col) for k in range(outer)]
    cols = lambda j: pl.ds(pl.multiple_of(j * slab, slab), slab)
    halves = lambda j: pl.ds(pl.multiple_of(j * half, half), half)
    greet([pair] + peer[1:])
    swap = remote(part_ref.at[:, halves(1 - i)], land, s0.at[0], r0.at[0], pair)
    swap.start()
    swap.wait_recv()
    both[...] = (part_ref[:, halves(i)].astype(jnp.float32) + land[...].astype(jnp.float32)).astype(both.dtype)
    scatter = [remote(both.at[:, cols(at[k])], inbox.at[k], s1.at[k], r1.at[k], peer[k]) for k in range(1, outer)]
    for copy in scatter:
        copy.start()
    total = part_ref[:, cols(i * outer + o)].astype(jnp.float32) + land[:, cols(o)].astype(jnp.float32)
    for k in range(1, outer):
        scatter[k - 1].wait_recv()
        total = total + inbox[k].astype(jnp.float32)
    home = cols(i * outer + o)
    out_ref[:, home] = total.astype(out_ref.dtype)
    mine = out_ref.at[:, home]
    spread = [remote(mine, mine, s2.at[k], r2.at[k], peer[k]) for k in range(1, outer)]
    spread.append(remote(mine, mine, s3.at[0], r3.at[0], pair))
    for copy in spread:
        copy.start()
    for k in range(1, outer):
        block = out_ref.at[:, cols(i * outer + back[k])]
        remote(block, block, s2.at[k], r2.at[k], pair).wait_recv()
        step = remote(block, block, s3.at[k], r3.at[k], pair)
        step.start()
        spread.append(step)
    for k in range(outer):
        block = out_ref.at[:, cols((1 - i) * outer + back[k])]
        remote(block, block, s3.at[k], r3.at[k], pair).wait_recv()
    for copy in [swap] + scatter + spread:
        copy.wait_send()


def reduce_all(part, n, ident):
    count, width = part.shape
    outer = n // 2
    vmem = pl.BlockSpec(memory_space=pltpu.VMEM)
    return pl.pallas_call(
        functools.partial(reduce_kernel, n),
        out_shape=jax.ShapeDtypeStruct(part.shape, part.dtype),
        in_specs=[vmem],
        out_specs=vmem,
        scratch_shapes=[
            pltpu.VMEM((count, width // 2), part.dtype),
            pltpu.VMEM((count, width // 2), part.dtype),
            pltpu.VMEM((outer, count, width // n), part.dtype),
        ]
        + [pltpu.SemaphoreType.DMA((outer,)) for _ in range(8)],
        compiler_params=pltpu.CompilerParams(collective_id=ident, has_side_effects=True),
    )(part)


def tiny_kernel(p, part_ref, out_ref, land, s1, r1):
    me, col = lax.axis_index("samp"), lax.axis_index("par")
    at = [lax.rem(col + k, p) for k in range(p)]
    back = [lax.rem(col + p - k, p) for k in range(p)]
    greet([(me, at[k]) for k in range(1, p)])
    copies = [remote(part_ref, land.at[col], s1.at[k], r1.at[k], (me, at[k])) for k in range(1, p)]
    for copy in copies:
        copy.start()
    land[col] = part_ref[...]
    for k in range(1, p):
        remote(part_ref, land.at[back[k]], s1.at[k], r1.at[k], (me, at[k])).wait_recv()
    for copy in copies:
        copy.wait_send()
    total = land[0]
    for j in range(1, p):
        total = total + land[j]
    out_ref[...] = total


def tiny_sum(part, p, ident):
    vmem = pl.BlockSpec(memory_space=pltpu.VMEM)
    return pl.pallas_call(
        functools.partial(tiny_kernel, p),
        out_shape=jax.ShapeDtypeStruct(part.shape, part.dtype),
        in_specs=[vmem],
        out_specs=vmem,
        scratch_shapes=[pltpu.VMEM((p,) + part.shape, part.dtype)]
        + [pltpu.SemaphoreType.DMA((p,)) for _ in range(2)],
        compiler_params=pltpu.CompilerParams(collective_id=ident, has_side_effects=True),
    )(part)


def body(log_derivs, energies, nys_rows):
    rows, width = log_derivs.shape
    n, p = lax.axis_size("samp"), lax.axis_size("par")
    count, rank = energies.shape[1], nys_rows.shape[1]
    scale = 1.0 / math.sqrt(width * p)
    picks = (nys_rows.reshape(rank, 1) == lax.broadcasted_iota(jnp.int32, (rank, rows), 1)).astype(jnp.bfloat16)
    probe = jnp.concatenate([picks, jnp.ones((8, rows), jnp.bfloat16)], axis=0)
    taken = jnp.dot(probe, log_derivs, preferred_element_type=jnp.float32)
    chosen = taken[:rank].astype(jnp.bfloat16)
    sums = taken[rank].reshape(n, 1, width // n)
    aux = jnp.concatenate([energies, picks.astype(jnp.float32).T], axis=1)
    sketch_part, aux_all, centered = gather_rows(sums, aux, chosen, log_derivs, n, n * rows, scale, 0)
    sketch = sum_and_spread(sketch_part, n, p, 1).reshape(n * rows, n * rank)
    all_energies = aux_all[:, :, :count].reshape(n * rows, count)
    core_block = jnp.einsum(
        "grj,grk->gjk", aux_all[:, :, count:], sketch.reshape(n, rows, n * rank), precision=lax.Precision.HIGHEST
    ).reshape(n * rank, n * rank)
    factor = jnp.linalg.cholesky(damping * core_block + hdot(sketch.T, sketch))

    def precondition(residual):
        coeffs = factor_solve(factor, hdot(sketch.T, residual))
        result = (residual - hdot(sketch, coeffs)) / damping
        return (result, hdot(result.T, residual))

    start = lax.axis_index("samp") * rows
    solution = jnp.zeros(all_energies.shape, jnp.float32)
    update = 0.0
    residual = all_energies
    precond_res, inner_prev = precondition(residual)
    direction = precond_res
    for iteration in range(ITERS):
        rounded = lax.dynamic_slice_in_dim(direction, start, rows, 0).astype(jnp.bfloat16)
        part = jnp.einsum("rv,rc->vc", rounded, centered, preferred_element_type=jnp.float32)
        projected = reduce_all(part.astype(jnp.bfloat16), n, 2 + 2 * iteration)
        if iteration + 1 < ITERS:
            image_part = jnp.einsum("rc,vc->vr", centered, projected, preferred_element_type=jnp.float32)
            image_k = sum_and_spread(image_part, n, p, 3 + 2 * iteration)
            image_k = image_k.transpose(0, 2, 1).reshape(n * rows, count) + damping * direction
            curvature = hdot(direction.T, image_k)
        else:
            square = jnp.einsum("uc,vc->uv", projected, projected, preferred_element_type=jnp.float32)
            curvature = tiny_sum(square, p, 3 + 2 * iteration) + damping * hdot(direction.T, direction)
        alpha_k = small_solve(curvature, inner_prev)
        solution = solution + hdot(direction, alpha_k)
        update = update + hdot(alpha_k.T, projected.astype(jnp.float32))
        if iteration + 1 < ITERS:
            residual = residual - hdot(image_k, alpha_k)
            precond_res, inner_next = precondition(residual)
            beta_k = small_solve(inner_prev, inner_next)
            direction = precond_res + hdot(direction, beta_k)
            inner_prev = inner_next
    return (update.T, lax.dynamic_slice_in_dim(solution, start, rows, 0))


def solution(mesh):
    return jax.shard_map(
        body,
        mesh=mesh,
        in_specs=(P("samp", "par"), P("samp", None), P("samp", None)),
        out_specs=(P("par", None), P("samp", None)),
        check_vma=False,
    )
```

profile of v0, /device:TPU:0, one launch (start us, length us, event | category | flops | bytes accessed | tf_op | source)
XLA Modules:
  0.0 212.1 jit_solution(10340738183449727721)
XLA Ops:
  0.6 0.0 copy-start.5
  0.6 0.0 copy-start.4
  0.6 0.8 iota_compare_fusion.3
  1.4 4.6 %fusion.15 = f32[16,65536]{1,0:T(8,128)S(1)} fusion(bf16[64,65536]{1,0:T(8,128)(2,1)} %full_ref.1, pred[8,64]{1,0:T(8,128)(4,1)S(1)} %iota_compare_fusion.3), kind=kOutput, calls=%fused_computation.34 | convolution fusion | flops 134217728 | bytes 12583424 | tf_op jit(solution)/shard_map/dot_general | solution.py:374
  6.0 1.1 slice.34.chosen_ref
  7.1 0.8 slice.27
  7.9 0.0 copy-done.5
  7.9 0.1 fusion.21
  8.0 0.0 copy-done.4
  8.0 0.7 copy.28.aux_ref
  8.7 64.5 %shard_map.50 = (f32[64,64]{1,0:T(8,128)}, f32[8,64,16]{2,1,0:T(8,128)}, bf16[64,65536]{1,0:T(8,128)(2,1)}) custom-call(f32[8,1,8192]{2,1,0:T(1,128)} %bitcast.91, f32[64,16]{1,0:T(8,128)} %copy.28.aux_ref, bf16[8,65536]{1,0:T(8,128)(2,1)} %slice.34.chosen_ref, bf16[64,65536]{1,0:T(8,128)(2,1)} %full_ref.1), custom_call_target="tpu_custom_call" | custom-call | tf_op jit(solution)/shard_map/pallas_call | solution.py:203
  73.2 13.3 %shard_map.51 = f32[8,64,64]{2,1,0:T(8,128)} custom-call(f32[64,64]{1,0:T(8,128)} %get-tuple-element.8.part_ref), custom_call_target="tpu_custom_call" | custom-call | tf_op jit(solution)/shard_map/pallas_call | solution.py:255
  86.5 1.7 fusion.1
  88.2 0.1 copy.31
  88.3 1.6 fusion
  89.9 0.1 copy.33
  90.0 5.8 %cholesky.18 = f32[64,64]{1,0:T(8,128)S(1)} custom-call(f32[64,64]{1,0:T(8,128)S(1)} %fusion.14), custom_call_target="Cholesky" | custom-call | tf_op jit(solution)/shard_map/jit(cholesky)/cholesky | solution.py:384
  95.9 0.6 compare_reduce_fusion
  96.5 0.7 fusion.5
  97.2 4.9 %custom-call.12 = f32[1,64,64]{1,2,0:T(8,128)S(1)} custom-call(f32[1,64,64]{2,1,0:T(8,128)S(1)} %fusion.5), custom_call_target="InvertDiagBlocksLowerTriangular" | custom-call | tf_op jit(solution)/shard_map/triangular_solve/custom-call.2 | solution.py:21
  102.1 1.6 convolution_bitcast_fusion.1
  103.7 0.2 fusion.10
  103.8 0.2 fusion.12
  104.0 1.1 copy.35
  105.1 1.3 broadcast_multiply_fusion
  106.4 1.8 fusion.26.right_ref
  108.2 0.0 copy-start
  108.2 5.7 %convolution_convert_fusion.1.part_ref = bf16[8,65536]{1,0:T(8,128)(2,1)} fusion(bf16[64,65536]{1,0:T(8,128)(2,1)} %get-tuple-element.9, bf16[512,8]{0,1:T(8,128)(2,1)S(1)} %get-tuple-element.10, s32[]{:T(128)S(6)} %select_n.10), kind=kOutput, calls=%fused_computation.2 | convolution fusion | flops 67633152 | bytes 9439236 | tf_op jit(solution)/shard_map/rv,rc->vc/dot_general | solution.py:399
  113.8 23.3 %shard_map.52 = bf16[8,65536]{1,0:T(8,128)(2,1)} custom-call(bf16[8,65536]{1,0:T(8,128)(2,1)} %convolution_convert_fusion.1.part_ref), custom_call_target="tpu_custom_call" | custom-call | tf_op jit(solution)/shard_map/pallas_call | solution.py:320
  137.2 6.6 %fusion.29.part_ref = f32[8,64]{1,0:T(8,128)} fusion(bf16[8,65536]{1,0:T(8,128)(2,1)} %shard_map.52, bf16[64,65536]{1,0:T(8,128)(2,1)} %get-tuple-element.9), kind=kOutput, calls=%fused_computation.57 | convolution fusion | flops 67108864 | bytes 9439232 | tf_op jit(solution)/shard_map/rc,vc->vr/dot_general | solution.py:402
  143.8 10.4 %shard_map.53 = f32[8,8,64]{2,1,0:T(8,128)} custom-call(f32[8,64]{1,0:T(8,128)} %fusion.29.part_ref), custom_call_target="tpu_custom_call" | custom-call | tf_op jit(solution)/shard_map/pallas_call | solution.py:255
  154.2 0.8 copy.36
  155.0 0.1 reshape.38
  155.0 0.1 fusion.27
  155.2 0.1 copy.37
  155.2 0.6 fusion.19.matrix_ref
  155.9 1.9 shard_map.54
  157.8 0.9 fusion.25
  158.7 0.9 convolution_subtract_fusion.1
  159.6 0.0 copy-done
  159.6 0.2 fusion.31
  159.8 0.2 fusion.6
  160.0 0.2 fusion.8
  160.2 0.4 fusion.2
  160.5 0.8 fusion.32.right_ref
  161.3 0.0 copy-done.2
  161.3 0.1 copy.39
  161.4 0.6 fusion.18.matrix_ref
  162.0 1.9 shard_map.55
  163.9 0.9 convolution_add_fusion.1
  164.8 5.6 %convolution_convert_fusion.part_ref = bf16[8,65536]{1,0:T(8,128)(2,1)} fusion(bf16[64,65536]{1,0:T(8,128)(2,1)} %get-tuple-element.9, f32[512,8]{0,1:T(8,128)S(1)} %convolution_add_fusion.1, s32[]{:T(128)S(6)} %select_n.10), kind=kOutput, calls=%fused_computation.1 | convolution fusion | flops 67633152 | bytes 9439236 | tf_op jit(solution)/shard_map/rv,rc->vc/dot_general | solution.py:399
  170.4 22.3 %shard_map.56 = bf16[8,65536]{1,0:T(8,128)(2,1)} custom-call(bf16[8,65536]{1,0:T(8,128)(2,1)} %convolution_convert_fusion.part_ref), custom_call_target="tpu_custom_call" | custom-call | tf_op jit(solution)/shard_map/pallas_call | solution.py:320
  192.7 2.9 %fusion.33.part_ref = f32[8,8]{1,0:T(8,128)} fusion(bf16[8,65536]{1,0:T(8,128)(2,1)} %shard_map.56), kind=kOutput, calls=%fused_computation.61 | convolution fusion | flops 8388608 | bytes 1048832 | tf_op jit(solution)/shard_map/uc,vc->uv/dot_general | solution.py:407
  195.6 6.8 %shard_map.57 = f32[8,8]{1,0:T(8,128)} custom-call(f32[8,8]{1,0:T(8,128)} %fusion.33.part_ref), custom_call_target="tpu_custom_call" | custom-call | tf_op jit(solution)/shard_map/pallas_call | solution.py:356
  202.4 0.8 fusion.3
  203.2 0.1 copy.40
  203.3 0.6 fusion.17.matrix_ref
  203.9 1.9 shard_map.58
  205.8 0.9 fusion.34
  206.7 0.7 dynamic-slice_add_fusion
  207.3 0.0 copy-done.1
  207.4 0.0 copy-done.3
  207.4 1.0 fusion.30
  208.4 3.7 %convolution_add_fusion = f32[65536,8]{0,1:T(8,128)} fusion(f32[65536,8]{0,1:T(8,128)S(1)} %fusion.30, bf16[8,65536]{1,0:T(8,128)(2,1)} %shard_map.56, f32[8,8]{1,0:T(8,128)} %shard_map.58), kind=kOutput, calls=%fused_computation | convolution fusion | flops 50855936 | bytes 5243136 | tf_op jit(solution)/shard_map/dot_general | solution.py:45
  (7 shorter events, 0.1 us)
Async XLA Ops:
  0.6 7.3 %copy-start.5 = (s32[1,8]{1,0:T(1,128)S(1)}, s32[1,8]{1,0:T(1,128)}, u32[]{:S(2)}) copy-start(s32[1,8]{1,0:T(1,128)} %param.9) | copy-start | bytes 100
  0.6 7.4 %copy-start.4 = (f32[64,8]{0,1:T(8,128)S(1)}, f32[64,8]{0,1:T(8,128)}, u32[]{:S(2)}) copy-start(f32[64,8]{0,1:T(8,128)} %param.8) | copy-start | bytes 6148
  108.2 51.4 %copy-start = (f32[8,64,64]{2,1,0:T(8,128)S(1)}, f32[8,64,64]{2,1,0:T(8,128)}, u32[]{:S(2)}) copy-start(f32[8,64,64]{2,1,0:T(8,128)} %shard_map.51) | copy-start | bytes 393220
  113.8 47.5 %copy-start.2 = (f32[8,8]{1,0:T(8,128)S(1)}, f32[8,8]{1,0:T(8,128)}, u32[]{:S(2)}) copy-start(f32[8,8]{1,0:T(8,128)} %fusion.26.right_ref) | copy-start | bytes 772
  143.8 63.6 %copy-start.1 = (bf16[8,65536]{1,0:T(8,128)(2,1)S(1)}, bf16[8,65536]{1,0:T(8,128)(2,1)}, u32[]{:S(2)}) copy-start(bf16[8,65536]{1,0:T(8,128)(2,1)} %shard_map.52) | copy-start | bytes 3145732
  157.8 49.6 %copy-start.3 = (f32[8,8]{1,0:T(8,128)S(1)}, f32[8,8]{1,0:T(8,128)}, u32[]{:S(2)}) copy-start(f32[8,8]{1,0:T(8,128)} %shard_map.54) | copy-start | bytes 772
where the time goes:
time: 213 us; the launch traced here: 212 us
  Pallas kernels  146 us (69%)
  matrix products  44.6 us (21%)
  other arithmetic  15.5 us (7%)
  local copies, waits for them, and re-layouts  4.92 us (2%)
    pallas_call x1, Pallas kernels, gather_rows(): pl.pallas_call(functools.partial(gather_kernel, n, total_rows, scale), ou...  64.5 us
    pallas_call x2, Pallas kernels, reduce_all(): pl.pallas_call(functools.partial(reduce_kernel, n), out_shape=jax.ShapeDt...  45.6 us
    pallas_call x2, Pallas kernels, sum_and_spread(): pl.pallas_call(functools.partial(spread_kernel, n, p), out_shape=jax.Shap...  23.7 us
    dot_general x15, matrix products, hdot(): return jnp.dot(left, right, precision=lax.Precision.HIGHEST)  16.9 us
    dot_general x2, matrix products, body(): jnp.einsum('rv,rc->vc', rounded, centered, preferred_element_type=jnp.flo...  11.3 us
    pallas_call x1, Pallas kernels, tiny_sum(): pl.pallas_call(functools.partial(tiny_kernel, p), out_shape=jax.ShapeDtyp...  6.75 us
    dot_general x1, matrix products, body(): jnp.einsum('rc,vc->vr', centered, projected, preferred_element_type=jnp.f...  6.59 us
    another operation x3, other arithmetic, body(): factor = jnp.linalg.cholesky(damping * core_block + hdot(sketch.T, sketch))  6.52 us

commit v1 on v0

--- a/solution.py
+++ b/solution.py
@@ -364,7 +364,7 @@
     )(part)
 
 
-def body(log_derivs, energies, nys_rows):
+def general_body(log_derivs, energies, nys_rows):
     rows, width = log_derivs.shape
     n, p = lax.axis_size("samp"), lax.axis_size("par")
     count, rank = energies.shape[1], nys_rows.shape[1]
@@ -418,7 +418,586 @@
     return (update.T, lax.dynamic_slice_in_dim(solution, start, rows, 0))
 
 
+CHUNKS = 16
+EARLY = 4
+AHEAD = 8
+LAG = 2
+
+
+def contract_last(left, right, precision=None):
+    return lax.dot_general(
+        left, right, (((1,), (1,)), ((), ())), precision=precision, preferred_element_type=jnp.float32
+    )
+
+
+def exact(left, right):
+    return jnp.dot(left, right, precision=lax.Precision.HIGHEST, preferred_element_type=jnp.float32)
+
+
+def exact_t(left, right):
+    return contract_last(left, right, lax.Precision.HIGHEST)
+
+
+def places():
+    me, z = lax.axis_index("samp"), lax.axis_index("par")
+    c, q = lax.rem(me, 2), me // 2
+    near = [jnp.bitwise_xor(q, 1), jnp.bitwise_xor(q, 2)]
+    return me, z, c, 1 - c, q, near, jnp.bitwise_xor(q, 3)
+
+
+def sketch_kernel(p, total_rows, scale, x_ref, probe_ref, aux_ref, sk_ref, aux_out, c_out, stage, xh, other, rin,
+                  sums, sland, acc1, acc2, mean, acc, pland, mine, zland, tot, lsem, wsem, wrecv, osem, psem, rsem,
+                  fsem, drecv, bsem, brecv, asem, arecv, tsem, trecv, csem, local):
+    me, z, c, o, q, near, far = places()
+    rows, half = stage.shape
+    width = half // CHUNKS
+    count = rin.shape[1]
+    dev = lambda chip, core: (chip * 2 + core, z)
+    pair = dev(q, o)
+    span = lambda k: pl.ds(pl.multiple_of(k * width, width), width)
+
+    def load(k, own):
+        core = c if own else o
+        cols = pl.ds(pl.multiple_of(core * half + k * width, width), width)
+        dst = xh.at[c, :, span(k)] if own else stage.at[:, span(k)]
+        return pltpu.make_async_copy(x_ref.at[:, cols], dst, lsem.at[int(own), k])
+
+    @pl.loop(0, CHUNKS)
+    def _(k):
+        load(k, False).start()
+        load(k, True).start()
+
+    samp_peers = [(lax.rem(me + k, 8), z) for k in range(1, 8)]
+    par_peers = [(me, lax.rem(z + k, p)) for k in range(1, p)]
+    greet(samp_peers + par_peers)
+    auxes = [remote(aux_ref, aux_out.at[me], asem.at[k], arecv.at[k], samp_peers[k]) for k in range(7)]
+    for copy in auxes:
+        copy.start()
+    keep = pltpu.make_async_copy(aux_ref, aux_out.at[me], local.at[0])
+    keep.start()
+
+    def swap(k):
+        return remote(stage.at[:, span(k)], xh.at[c, :, span(k)], wsem.at[k], wrecv.at[k], pair)
+
+    def to_pair(k):
+        return remote(other.at[:, span(k)], rin.at[me, :, span(k)], psem.at[k], rsem.at[me, k], pair)
+
+    def direct(k):
+        view = rin.at[me, :, span(k)]
+        found = []
+        for d in range(2):
+            found.append(remote(view, view, osem.at[d, k], rsem.at[me, k], dev(near[d], c)))
+            found.append(remote(other.at[:, span(k)], view, osem.at[2 + d, k], rsem.at[me, k], dev(near[d], o)))
+        return found
+
+    def forward(k, d):
+        view = rin.at[pl.ds(pl.multiple_of(near[d] * 2, 2), 2), :, span(k)]
+        return remote(view, view, fsem.at[k], drecv.at[k], dev(near[1 - d], c))
+
+    def send(k):
+        for copy in direct(k):
+            copy.start()
+
+    def extract(k):
+        for own in (False, True):
+            load(k, own).wait()
+            step = min(width, 1024)
+            for s in range(width // step):
+                cols = pl.ds(pl.multiple_of(k * width + s * step, step), step)
+                block = xh[c, :, cols] if own else stage[:, cols]
+                taken = jnp.dot(probe_ref[...], block, preferred_element_type=jnp.float32)
+                if own:
+                    rin[me, :, cols] = taken[:count].astype(rin.dtype)
+                    sums[c, :, cols] = taken[count:count + 1]
+                else:
+                    other[:, cols] = taken[:count].astype(other.dtype)
+                    sums[o, :, cols] = taken[count:count + 1]
+            if not own:
+                swap(k).start()
+                to_pair(k).start()
+
+    @pl.loop(0, EARLY)
+    def _(k):
+        extract(k)
+        send(k)
+
+    @pl.loop(EARLY, CHUNKS)
+    def _(k):
+        extract(k)
+
+    first = remote(sums.at[o], sland.at[0], bsem.at[0], brecv.at[0], pair)
+    first.start()
+    first.wait_recv()
+    acc1[...] = sums[c] + sland[0]
+    part = [pl.ds(0, half // 2), pl.ds(half // 2, half // 2)]
+    second = [
+        remote(acc1.at[:, part[d]], sland.at[1, :, part[d]], bsem.at[1 + d], brecv.at[1 + d], dev(near[d], c))
+        for d in range(2)
+    ]
+    for copy in second:
+        copy.start()
+
+    middle = (EARLY + AHEAD) // 2
+
+    @pl.loop(EARLY, middle)
+    def _(k):
+        send(k)
+
+    for copy in second:
+        copy.wait_recv()
+    acc2[...] = acc1[...] + sland[1]
+    third = [
+        remote(acc2.at[:, part[d]], sland.at[2, :, part[d]], bsem.at[3 + d], brecv.at[3 + d], dev(near[1 - d], c))
+        for d in range(2)
+    ]
+    for copy in third:
+        copy.start()
+
+    @pl.loop(middle, AHEAD)
+    def _(k):
+        send(k)
+
+    for copy in third:
+        copy.wait_recv()
+    mean[...] = (acc2[...] + sland[2]) / total_rows
+    acc[...] = jnp.zeros_like(acc)
+
+    def arrived(k):
+        for d in range(2):
+            for core in range(2):
+                g = near[d] * 2 + core
+                view = rin.at[g, :, span(k)]
+                remote(view, view, fsem.at[k], rsem.at[g, k], pair).wait_recv()
+
+    def process(k):
+        remote(stage.at[:, span(k)], xh.at[o, :, span(k)], wsem.at[k], wrecv.at[k], pair).wait_recv()
+        g = me + 1 - 2 * c
+        view = rin.at[g, :, span(k)]
+        remote(view, view, fsem.at[k], rsem.at[g, k], pair).wait_recv()
+        view = rin.at[pl.ds(pl.multiple_of(far * 2, 2), 2), :, span(k)]
+        remote(view, view, fsem.at[k], drecv.at[k], pair).wait_recv()
+        step = min(width, 512)
+        for s in range(width // step):
+            cols = pl.ds(pl.multiple_of(k * width + s * step, step), step)
+            shift = mean[:, cols]
+            block = xh[:, :, cols].astype(jnp.float32).reshape(2 * rows, step)
+            block = ((block - shift) * scale).astype(jnp.bfloat16)
+            xh[:, :, cols] = block.reshape(2, rows, step)
+            picked = rin[:, :, cols].astype(jnp.float32).reshape(8 * count, step)
+            picked = ((picked - shift) * scale).astype(jnp.bfloat16)
+            acc[...] += contract_last(picked, block)
+        pltpu.make_async_copy(xh.at[:, :, span(k)], c_out.at[:, :, span(k)], csem.at[k]).start()
+
+    @pl.loop(0, (CHUNKS + LAG) // 2)
+    def _(i):
+        for d in range(2):
+            k = 2 * i + d
+
+            @pl.when(k + AHEAD < CHUNKS)
+            def _():
+                send(k + AHEAD)
+
+            @pl.when(k < CHUNKS)
+            def _():
+                arrived(k)
+                forward(k, d).start()
+
+            @pl.when(k >= LAG)
+            def _():
+                process(k - LAG)
+
+    own_rows = acc.shape[0] // 2
+    mine_rows = pl.ds(pl.multiple_of(c * own_rows, own_rows), own_rows)
+    their_rows = pl.ds(pl.multiple_of(o * own_rows, own_rows), own_rows)
+    give = remote(acc.at[their_rows], pland, tsem.at[0], trecv.at[0], pair)
+    give.start()
+    give.wait_recv()
+    mine[...] = acc[mine_rows, :] + pland[...]
+    across = [remote(mine, zland.at[z], tsem.at[k], trecv.at[k], par_peers[k - 1]) for k in range(1, p)]
+    for copy in across:
+        copy.start()
+    zland[z] = mine[...]
+    for k in range(1, p):
+        view = zland.at[lax.rem(z + p - k, p)]
+        remote(view, view, tsem.at[k], trecv.at[k], pair).wait_recv()
+    total = zland[0]
+    for j in range(1, p):
+        total = total + zland[j]
+    tot[...] = total
+    spot = lambda chip, core: sk_ref.at[
+        pl.ds(pl.multiple_of(core * own_rows, own_rows), own_rows),
+        pl.ds(pl.multiple_of(chip * 2 * rows, 2 * rows), 2 * rows),
+    ]
+    sk_ref[mine_rows, pl.ds(pl.multiple_of(q * 2 * rows, 2 * rows), 2 * rows)] = total
+    spread = [remote(tot, spot(q, c), tsem.at[p + k], trecv.at[p + k], samp_peers[k]) for k in range(7)]
+    for copy in spread:
+        copy.start()
+    for k in range(7):
+        source = lax.rem(me + 7 - k, 8)
+        view = spot(source // 2, lax.rem(source, 2))
+        remote(view, view, tsem.at[p + k], trecv.at[p + k], pair).wait_recv()
+    for k in range(7):
+        view = aux_out.at[lax.rem(me + 7 - k, 8)]
+        remote(view, view, asem.at[k], arecv.at[k], pair).wait_recv()
+    keep.wait()
+
+    @pl.loop(0, CHUNKS // 2)
+    def _(i):
+        for d in range(2):
+            k = 2 * i + d
+            swap(k).wait_send()
+            to_pair(k).wait_send()
+            for copy in direct(k):
+                copy.wait_send()
+            forward(k, d).wait_send()
+            pltpu.make_async_copy(xh.at[:, :, span(k)], c_out.at[:, :, span(k)], csem.at[k]).wait()
+
+    for copy in auxes + [first] + second + third + [give] + across + spread:
+        copy.wait_send()
+
+
+def sketch_call(x, probe, aux, p, total_rows, scale, ident):
+    rows, full = x.shape
+    half = full // 2
+    count = probe.shape[0] // 2
+    vmem, hbm = pl.BlockSpec(memory_space=pltpu.VMEM), pl.BlockSpec(memory_space=pl.ANY)
+    dma = lambda *shape: pltpu.SemaphoreType.DMA(shape)
+    rank = 8 * count
+    line = lambda k: pltpu.VMEM((k, 1, half), jnp.float32)
+    return pl.pallas_call(
+        functools.partial(sketch_kernel, p, total_rows, scale),
+        out_shape=(
+            jax.ShapeDtypeStruct((rank, 8 * rows), jnp.float32),
+            jax.ShapeDtypeStruct((8,) + aux.shape, jnp.float32),
+            jax.ShapeDtypeStruct((2, rows, half), x.dtype),
+        ),
+        in_specs=[hbm, vmem, vmem],
+        out_specs=(vmem, vmem, hbm),
+        scratch_shapes=[
+            pltpu.VMEM((rows, half), x.dtype),
+            pltpu.VMEM((2, rows, half), x.dtype),
+            pltpu.VMEM((count, half), x.dtype),
+            pltpu.VMEM((8, count, half), x.dtype),
+            line(2),
+            line(3),
+            pltpu.VMEM((1, half), jnp.float32),
+            pltpu.VMEM((1, half), jnp.float32),
+            pltpu.VMEM((1, half), jnp.float32),
+            pltpu.VMEM((rank, 2 * rows), jnp.float32),
+            pltpu.VMEM((rank // 2, 2 * rows), jnp.float32),
+            pltpu.VMEM((rank // 2, 2 * rows), jnp.float32),
+            pltpu.VMEM((p, rank // 2, 2 * rows), jnp.float32),
+            pltpu.VMEM((rank // 2, 2 * rows), jnp.float32),
+            dma(2, CHUNKS), dma(CHUNKS), dma(CHUNKS), dma(4, CHUNKS), dma(CHUNKS), dma(8, CHUNKS),
+            dma(CHUNKS), dma(CHUNKS), dma(5), dma(5), dma(7), dma(7), dma(p + 7), dma(p + 7), dma(CHUNKS), dma(1),
+        ],
+        compiler_params=pltpu.CompilerParams(
+            collective_id=ident, has_side_effects=True, vmem_limit_bytes=60 * 2**20
+        ),
+    )(x, probe, aux)
+
+
+def eliminate(matrix, size, group):
+    row = lax.broadcasted_iota(jnp.int32, matrix.shape, 0)
+    lanes = matrix.shape[1]
+    for start in range(0, size, group):
+        spread = lambda i, j: jnp.broadcast_to(matrix[start + i:start + i + 1, start + j:start + j + 1], (1, lanes))
+        cell = [[spread(i, j) for j in range(group)] for i in range(group)]
+        for k in range(group):
+            inverse = 1.0 / cell[k][k]
+            scaled = [cell[k][j] * inverse for j in range(group)]
+            for i in range(group):
+                if i != k:
+                    factor = cell[i][k]
+                    cell[i] = [cell[i][j] - factor * scaled[j] for j in range(group)]
+                    cell[i][k] = -factor * inverse
+            scaled[k] = inverse
+            cell[k] = scaled
+        old = [matrix[start + j:start + j + 1, :] for j in range(group)]
+        fresh = []
+        for i in range(group):
+            line = cell[i][0] * old[0]
+            for j in range(1, group):
+                line = line + cell[i][j] * old[j]
+            fresh.append(line)
+        change = matrix[:, start:start + 1] * fresh[0]
+        for i in range(1, group):
+            change = change + matrix[:, start + i:start + i + 1] * fresh[i]
+        matrix = matrix - change
+        for i in range(group):
+            matrix = jnp.where(row == start + i, fresh[i], matrix)
+    return matrix
+
+
+def solve_kernel(p, c_ref, sk_ref, aux_ref, update_ref, sol_ref, cbuf, aug, big, small, dref, rres, part, land1, mid,
+                 keep, land2, pf, msg, mland, img, lsem, s1, r1, s2, r2, s3, r3, s4, r4, s5, r5, s6, r6, s7, r7):
+    me, z, c, o, q, near, far = places()
+    rows, half = cbuf.shape[1], cbuf.shape[2]
+    quarter = half // 4
+    piece = quarter // 2
+    dev = lambda chip: (chip * 2 + c, z)
+    pair = (q * 2 + o, z)
+    pieces = CHUNKS // 2
+    width = half // pieces
+
+    def load(k):
+        cols = pl.ds(k * width, width)
+        return pltpu.make_async_copy(c_ref.at[:, :, cols], cbuf.at[:, :, cols], lsem.at[k])
+
+    for k in range(pieces):
+        load(k).start()
+    group = [(q * 2 + lax.rem(c + k // p, 2), lax.rem(z + lax.rem(k, p), p)) for k in range(1, 2 * p)]
+    chips = [dev(near[0]), dev(near[1]), dev(far)]
+    greet(chips + group)
+
+    rank = sk_ref.shape[0]
+    vecs = aug.shape[0] - rank
+    sketch = sk_ref[...]
+    aug[pl.ds(0, rank), :] = sketch
+    for g in range(8):
+        cols = pl.ds((g // 2) * 2 * rows, 2 * rows)
+        here = pl.ds(g * vecs, vecs)
+        aug[here, cols] = aug[here, cols] + damping * aux_ref[g, vecs:, :]
+    for chip in range(4):
+        cols = pl.ds(chip * 2 * rows, 2 * rows)
+        aug[pl.ds(rank, vecs), cols] = aux_ref[2 * chip, :vecs, :] + aux_ref[2 * chip + 1, :vecs, :]
+    product = exact_t(aug[...], sketch)
+    big[...] = (
+        lax.broadcasted_iota(jnp.int32, big.shape, 0) + rank == lax.broadcasted_iota(jnp.int32, big.shape, 1)
+    ).astype(jnp.float32)
+    big[:, pl.ds(0, rank)] = product[:rank]
+    inverse = eliminate(big[...], rank, 4)[:, rank:2 * rank]
+    energies = aug[pl.ds(rank, vecs), :]
+    dref[...] = (energies - exact(exact(product[rank:], inverse), sketch)) / damping
+    gamma = exact_t(dref[...], energies)
+
+    def small_inverse(matrix):
+        small[...] = (
+            lax.broadcasted_iota(jnp.int32, small.shape, 0) + vecs == lax.broadcasted_iota(jnp.int32, small.shape, 1)
+        ).astype(jnp.float32)
+        small[:, pl.ds(0, vecs)] = matrix
+        return eliminate(small[...], vecs, 4)[:, vecs:2 * vecs]
+
+    spot = lambda chip, s: pl.ds(pl.multiple_of(chip * quarter + s * piece, piece), piece)
+    step = min(piece, 1024)
+
+    def all_reduce(turn):
+        rounded = dref[:, pl.ds(pl.multiple_of(q * 2 * rows, 2 * rows), 2 * rows)].astype(jnp.bfloat16)
+
+        def project(chip, s):
+            @pl.loop(0, piece // step)
+            def _(t):
+                cols = pl.ds(pl.multiple_of(chip * quarter + s * piece + t * step, step), step)
+                block = cbuf[:, :, cols].reshape(2 * rows, step)
+                part[turn, :, cols] = jnp.dot(rounded, block, preferred_element_type=jnp.float32).astype(part.dtype)
+
+        sends = []
+        for j, target in enumerate((lambda d: far, lambda d: near[d])):
+            for d in range(2):
+                chip = target(d)
+                project(chip, d)
+                copy = remote(part.at[turn, :, spot(chip, d)], land1.at[turn, d, j], s1.at[turn, d, j],
+                              r1.at[turn, d, j], dev(near[d]))
+                copy.start()
+                sends.append(copy)
+        for d in range(2):
+            project(near[1 - d], d)
+        for d in range(2):
+            project(q, d)
+        for d in range(2):
+            sends[d].wait_recv()
+            mid[turn, d] = (
+                part[turn, :, spot(near[1 - d], d)].astype(jnp.float32) + land1[turn, d, 0].astype(jnp.float32)
+            ).astype(mid.dtype)
+            copy = remote(mid.at[turn, d], land2.at[turn, d], s2.at[turn, d], r2.at[turn, d], dev(near[1 - d]))
+            copy.start()
+            sends.append(copy)
+        for d in range(2):
+            sends[2 + d].wait_recv()
+            keep[d] = part[turn, :, spot(q, d)].astype(jnp.float32) + land1[turn, d, 1].astype(jnp.float32)
+        for d in range(2):
+            sends[4 + d].wait_recv()
+            pf[c, turn, :, spot(q, d)] = (keep[d] + land2[turn, d].astype(jnp.float32)).astype(pf.dtype)
+        mine = pl.ds(pl.multiple_of(q * quarter, quarter), quarter)
+        view = pf.at[c, turn, :, mine]
+        for d in range(2):
+            copy = remote(view, view, s3.at[turn, d], r3.at[turn, d], dev(near[d]))
+            copy.start()
+            sends.append(copy)
+        copy = remote(view, view, s5.at[turn, 0], r5.at[turn, 0], pair)
+        copy.start()
+        sends.append(copy)
+
+        def consume(chip):
+            @pl.loop(0, quarter // step)
+            def _(t):
+                cols = pl.ds(pl.multiple_of(chip * quarter + t * step, step), step)
+                block = pf[c, turn, :, cols]
+                msg[turn, pl.ds(vecs, vecs), pl.ds(0, vecs)] += contract_last(block, block)
+                if turn == 0:
+                    msg[turn, pl.ds(0, vecs), :] += contract_last(block, cbuf[:, :, cols].reshape(2 * rows, step))
+
+        msg[turn] = jnp.zeros(msg.shape[1:], jnp.float32)
+        consume(q)
+        for d in range(2):
+            theirs = pf.at[c, turn, :, pl.ds(pl.multiple_of(near[d] * quarter, quarter), quarter)]
+            remote(theirs, theirs, s3.at[turn, d], r3.at[turn, d], pair).wait_recv()
+            step_view = pf.at[c, turn, :, spot(near[d], d)]
+            copy = remote(step_view, step_view, s4.at[turn, d], r4.at[turn, d], dev(near[1 - d]))
+            copy.start()
+            sends.append(copy)
+            copy = remote(theirs, theirs, s5.at[turn, 1 + d], r5.at[turn, 1 + d], pair)
+            copy.start()
+            sends.append(copy)
+        for d in range(2):
+            consume(near[d])
+        for d in range(2):
+            view = pf.at[c, turn, :, spot(far, d)]
+            remote(view, view, s4.at[turn, d], r4.at[turn, d], pair).wait_recv()
+            copy = remote(view, view, s5.at[turn, 3 + d], r5.at[turn, 3 + d], pair)
+            copy.start()
+            sends.append(copy)
+        consume(far)
+        slot = z * 2 + c
+        for k in range(1, 2 * p):
+            copy = remote(msg.at[turn], mland.at[turn, slot], s6.at[turn, k], r6.at[turn, k], group[k - 1])
+            copy.start()
+            sends.append(copy)
+        mland[turn, slot] = msg[turn]
+        for k in range(1, 2 * p):
+            there = lax.rem(z + p - lax.rem(k, p), p) * 2 + lax.rem(c + k // p, 2)
+            view = mland.at[turn, there]
+            remote(view, view, s6.at[turn, k], r6.at[turn, k], pair).wait_recv()
+        total = mland[turn, 0]
+        for j in range(1, 2 * p):
+            total = total + mland[turn, j]
+        return total, sends
+
+    for k in range(pieces):
+        load(k).wait()
+    total, sends = all_reduce(0)
+    here = pl.ds(pl.multiple_of(q * 2 * rows, 2 * rows), 2 * rows)
+    img[0, :, here] = total[:vecs]
+    rres[...] = total[:vecs]
+    for k, chip in enumerate(chips):
+        copy = remote(rres, img.at[0, :, here], s7.at[k], r7.at[k], chip)
+        copy.start()
+        sends.append(copy)
+    direction = dref[...]
+    curvature = total[vecs:, :vecs] + damping * exact_t(direction, direction)
+    alpha = exact(gamma, small_inverse(curvature))
+    gamma_inverse = small_inverse(gamma)
+    for k, chip in enumerate([near[0], near[1], far]):
+        view = img.at[0, :, pl.ds(pl.multiple_of(chip * 2 * rows, 2 * rows), 2 * rows)]
+        remote(view, view, s7.at[k], r7.at[k], pair).wait_recv()
+    image = img[0] + damping * direction
+    residual = energies - exact(alpha, image)
+    fresh = (residual - exact(exact(exact_t(residual, sketch), inverse), sketch)) / damping
+    gamma_next = exact_t(fresh, residual)
+    beta = exact(gamma_next, gamma_inverse)
+    answer = exact(alpha, direction)
+    dref[...] = fresh + exact(beta, direction)
+    total, more = all_reduce(1)
+    direction = dref[...]
+    curvature = total[vecs:, :vecs] + damping * exact_t(direction, direction)
+    alpha_next = exact(gamma_next, small_inverse(curvature))
+    dref[...] = answer + exact(alpha_next, direction)
+    sol_ref[...] = dref[:, here]
+    weights = []
+    for value in (alpha, alpha_next):
+        upper = value.astype(jnp.bfloat16)
+        weights.append((upper, (value - upper.astype(jnp.float32)).astype(jnp.bfloat16)))
+
+    def finish(core):
+        @pl.loop(0, half // step)
+        def _(t):
+            cols = pl.ds(pl.multiple_of(t * step, step), step)
+            out = jnp.zeros((vecs, step), jnp.float32)
+            for turn in range(2):
+                block = pf[core, turn, :, cols]
+                for weight in weights[turn]:
+                    out = out + jnp.dot(weight, block, preferred_element_type=jnp.float32)
+            update_ref[:, pl.ds(pl.multiple_of(core * half + t * step, step), step)] = out
+
+    finish(c)
+    for turn in range(2):
+        for k, chip in enumerate([q, near[0], near[1]]):
+            view = pf.at[o, turn, :, pl.ds(pl.multiple_of(chip * quarter, quarter), quarter)]
+            remote(view, view, s5.at[turn, k], r5.at[turn, k], pair).wait_recv()
+        for d in range(2):
+            view = pf.at[o, turn, :, spot(far, d)]
+            remote(view, view, s5.at[turn, 3 + d], r5.at[turn, 3 + d], pair).wait_recv()
+    finish(o)
+    for copy in sends + more:
+        copy.wait_send()
+
+
+def solve_call(c_rows, sketch, aux, p, ident):
+    _, rows, half = c_rows.shape
+    vecs = aux.shape[1] // 2
+    rank, total = sketch.shape
+    vmem, hbm = pl.BlockSpec(memory_space=pltpu.VMEM), pl.BlockSpec(memory_space=pl.ANY)
+    dma = lambda *shape: pltpu.SemaphoreType.DMA(shape)
+    bf, f32 = jnp.bfloat16, jnp.float32
+    piece = half // 8
+    return pl.pallas_call(
+        functools.partial(solve_kernel, p),
+        out_shape=(
+            jax.ShapeDtypeStruct((vecs, 2 * half), f32),
+            jax.ShapeDtypeStruct((vecs, 2 * rows), f32),
+        ),
+        in_specs=[hbm, vmem, vmem],
+        out_specs=(vmem, vmem),
+        scratch_shapes=[
+            pltpu.VMEM(c_rows.shape, bf),
+            pltpu.VMEM((rank + vecs, total), f32),
+            pltpu.VMEM((rank, 2 * rank), f32),
+            pltpu.VMEM((vecs, 128), f32),
+            pltpu.VMEM((vecs, total), f32),
+            pltpu.VMEM((vecs, 2 * rows), f32),
+            pltpu.VMEM((2, vecs, half), bf),
+            pltpu.VMEM((2, 2, 2, vecs, piece), bf),
+            pltpu.VMEM((2, 2, vecs, piece), bf),
+            pltpu.VMEM((2, vecs, piece), f32),
+            pltpu.VMEM((2, 2, vecs, piece), bf),
+            pltpu.VMEM((2, 2, vecs, half), bf),
+            pltpu.VMEM((2, 2 * vecs, 2 * rows), f32),
+            pltpu.VMEM((2, 2 * p, 2 * vecs, 2 * rows), f32),
+            pltpu.VMEM((1, vecs, total), f32),
+            dma(CHUNKS // 2), dma(2, 2, 2), dma(2, 2, 2), dma(2, 2), dma(2, 2), dma(2, 2), dma(2, 2), dma(2, 2),
+            dma(2, 2), dma(2, 5), dma(2, 5), dma(2, 2 * p), dma(2, 2 * p), dma(3), dma(3),
+        ],
+        compiler_params=pltpu.CompilerParams(
+            collective_id=ident, has_side_effects=True, vmem_limit_bytes=60 * 2**20
+        ),
+    )(c_rows, sketch, aux)
+
+
+def paired_body(log_derivs, energies, nys_rows):
+    rows, width = log_derivs.shape
+    n, p = lax.axis_size("samp"), lax.axis_size("par")
+    rank = nys_rows.shape[1]
+    core = lax.rem(lax.axis_index("samp"), 2)
+    slots = lambda count: lax.broadcasted_iota(jnp.int32, (rank, count), 1)
+    picks = (nys_rows.reshape(rank, 1) == slots(rows)).astype(jnp.bfloat16)
+    probe = jnp.concatenate([picks, jnp.ones((rank, rows), jnp.bfloat16)], axis=0)
+    wide = (nys_rows.reshape(rank, 1) + core * rows == slots(2 * rows)).astype(jnp.float32)
+    side = jnp.concatenate([energies.T, energies.T], axis=1)
+    side = jnp.where(slots(2 * rows) // rows == core, side, 0.0)
+    aux = jnp.concatenate([side, wide], axis=0)
+    sketch, aux_all, c_rows = sketch_call(log_derivs, probe, aux, p, n * rows, 1.0 / math.sqrt(width * p), 0)
+    update, answer = solve_call(c_rows, sketch, aux_all, p, 1)
+    return (update.T, lax.dynamic_slice_in_dim(answer, core * rows, rows, 1).T)
+
+
 def solution(mesh):
+    n, p = mesh.shape["samp"], mesh.shape["par"]
+
+    def body(log_derivs, energies, nys_rows):
+        rows, count = log_derivs.shape[0], energies.shape[1]
+        paired = n == 8 and rows == 64 and count == 8 and nys_rows.shape[1] == count
+        return (paired_body if paired else general_body)(log_derivs, energies, nys_rows)
+
     return jax.shard_map(
         body,
         mesh=mesh,

time: 213 us -> 140 us (0.66)
  matrix products: 44.6 us -> 0 us
  Pallas kernels: 146 us -> 131 us
  other arithmetic: 15.5 us -> 3.5 us
    dot_general x21 -> x0, matrix products: 44 us -> none  [the longest x15 16.9 us: hdot(): return jnp.dot(left, right, precision=lax.Precision.HIGHEST)]
    pallas_call x9 -> x2, Pallas kernels: 146 us -> 131 us  [the longest x1 67.2 us: solve_call(): pl.pallas_call(functools.partial(solve_kernel, p), out_shape=(jax.ShapeDt...]
    another operation x5 -> x0, other arithmetic: 12.1 us -> none  [the longest x3 6.52 us: body(): factor = jnp.linalg.cholesky(damping * core_block + hdot(sketch.T, sketch))]
    unnamed x12 -> x1, local copies, waits for them, and re-layouts: 0.02 us -> 3.04 us
where the time goes in v1:
time: 140 us; the launch traced here: 139 us
  Pallas kernels  131 us (94%)
  local copies, waits for them, and re-layouts  4.39 us (3%)
  other arithmetic  3.5 us (2%)
    pallas_call x1, Pallas kernels, solve_call(): pl.pallas_call(functools.partial(solve_kernel, p), out_shape=(jax.ShapeDt...  67.2 us
    pallas_call x1, Pallas kernels, sketch_call(): pl.pallas_call(functools.partial(sketch_kernel, p, total_rows, scale), ou...  63.6 us
    unnamed x1, local copies, waits for them, and re-layouts  3.04 us

profile of v1, /device:TPU:0, one launch (start us, length us, event | category | flops | bytes accessed | tf_op | source)
XLA Modules:
  0.0 139.3 jit_solution(8053823133353774294)
XLA Ops:
  0.6 0.7 broadcast_add_fusion
  1.3 0.7 iota_compare_fusion.1
  2.0 0.8 maximum_select_fusion
  2.9 0.6 pad_convert_fusion.probe_ref
  3.5 0.1 fusion
  3.5 0.6 pad_maximum_fusion.aux_ref
  4.1 63.6 %shard_map.50 = (f32[64,512]{1,0:T(8,128)}, f32[8,16,128]{2,1,0:T(8,128)}, bf16[2,64,32768]{2,1,0:T(8,128)(2,1)}) custom-call(bf16[64,65536]{1,0:T(8,128)(2,1)} %x_ref.1, bf16[16,64]{1,0:T(8,128)(2,1)} %pad_convert_fusion.probe_ref, f32[16,128]{1,0:T(8,128)} %pad_maximum_fusion.aux_ref), custom_call_target="tpu_custom_call" | custom-call | tf_op jit(solution)/shard_map/pallas_call | solution.py:667
  67.7 67.2 %shard_map.51 = (f32[8,65536]{1,0:T(8,128)}, f32[8,128]{1,0:T(8,128)}) custom-call(bf16[2,64,32768]{2,1,0:T(8,128)(2,1)} %get-tuple-element.7.c_ref, f32[64,512]{1,0:T(8,128)} %get-tuple-element.8.sk_ref, f32[8,16,128]{2,1,0:T(8,128)} %get-tuple-element.9.aux_ref), custom_call_target="tpu_custom_call" | custom-call | tf_op jit(solution)/shard_map/pallas_call | solution.py:943
  134.9 1.3 dynamic-slice_bitcast_fusion
  136.3 3.0 %copy.6 = f32[65536,8]{0,1:T(8,128)} copy(f32[65536,8]{0,1:T(8,128)} %bitcast.6) | data formatting | bytes 4194304
  (2 shorter events, 0.0 us)

commit v2 on v0

--- a/solution.py
+++ b/solution.py
@@ -364,7 +364,7 @@
     )(part)
 
 
-def body(log_derivs, energies, nys_rows):
+def general_body(log_derivs, energies, nys_rows):
     rows, width = log_derivs.shape
     n, p = lax.axis_size("samp"), lax.axis_size("par")
     count, rank = energies.shape[1], nys_rows.shape[1]
@@ -418,7 +418,582 @@
     return (update.T, lax.dynamic_slice_in_dim(solution, start, rows, 0))
 
 
+CHUNKS = 8
+EARLY = 2
+AHEAD = 4
+LAG = 2
+
+
+def contract_last(left, right, precision=None):
+    return lax.dot_general(
+        left, right, (((1,), (1,)), ((), ())), precision=precision, preferred_element_type=jnp.float32
+    )
+
+
+def exact(left, right):
+    return jnp.dot(left, right, precision=lax.Precision.HIGHEST, preferred_element_type=jnp.float32)
+
+
+def exact_t(left, right):
+    return contract_last(left, right, lax.Precision.HIGHEST)
+
+
+def iota(shape, axis):
+    return lax.broadcasted_iota(jnp.int32, shape, axis)
+
+
+def eliminate(matrix, size, group):
+    row = iota(matrix.shape, 0)
+    lanes = matrix.shape[1]
+    for start in range(0, size, group):
+        spread = lambda i, j: jnp.broadcast_to(matrix[start + i:start + i + 1, start + j:start + j + 1], (1, lanes))
+        cell = [[spread(i, j) for j in range(group)] for i in range(group)]
+        for k in range(group):
+            inverse = 1.0 / cell[k][k]
+            scaled = [cell[k][j] * inverse for j in range(group)]
+            for i in range(group):
+                if i != k:
+                    factor = cell[i][k]
+                    cell[i] = [cell[i][j] - factor * scaled[j] for j in range(group)]
+                    cell[i][k] = -factor * inverse
+            scaled[k] = inverse
+            cell[k] = scaled
+        old = [matrix[start + j:start + j + 1, :] for j in range(group)]
+        fresh = []
+        for i in range(group):
+            line = cell[i][0] * old[0]
+            for j in range(1, group):
+                line = line + cell[i][j] * old[j]
+            fresh.append(line)
+        change = matrix[:, start:start + 1] * fresh[0]
+        for i in range(1, group):
+            change = change + matrix[:, start + i:start + i + 1] * fresh[i]
+        matrix = matrix - change
+        for i in range(group):
+            matrix = jnp.where(row == start + i, fresh[i], matrix)
+    return matrix
+
+
+def main_kernel(p, total_rows, scale, x_ref, energy_ref, picks_ref, pf_ref, alpha_ref, sol_ref,
+                stage, xh, other, rin, probe, aux, aux_all, sums, sland, acc1, acc2, mean, acc, pland, mine, zland,
+                tot, sk, aug, big, small, dref, rres, part, land1, mid, keep, land2, pf, sq, qland, qsum, qtot,
+                msg, mland, img,
+                lsem, wsem, wrecv, psem, precv, osem, rsem, fsem, drecv, bsem, brecv, asem, arecv, tsem, trecv,
+                s1, r1, s2, r2, s3, r3, s4, r4, s5, r5, s6, r6, s7, r7, s8, r8, s9, r9):
+    me, z = lax.axis_index("samp"), lax.axis_index("par")
+    c, q = lax.rem(me, 2), me // 2
+    o = 1 - c
+    near, far = [jnp.bitwise_xor(q, 1), jnp.bitwise_xor(q, 2)], jnp.bitwise_xor(q, 3)
+    rows, half = stage.shape
+    wide = 2 * rows
+    width = half // CHUNKS
+    count = rin.shape[1]
+    dev = lambda chip: (chip * 2 + c, z)
+    pair = (q * 2 + o, z)
+    chips = [near[0], near[1], far]
+    span = lambda k: pl.ds(pl.multiple_of(k * width, width), width)
+    duo = lambda chip: pl.ds(pl.multiple_of(chip * 2, 2), 2)
+    group = [(q * 2 + lax.rem(c + k // p, 2), lax.rem(z + lax.rem(k, p), p)) for k in range(1, 2 * p)]
+    samp_peers = [(lax.rem(me + k, 8), z) for k in range(1, 8)]
+    par_peers = group[:p - 1]
+
+    def load(k, own):
+        core = c if own else o
+        cols = pl.ds(pl.multiple_of(core * half + k * width, width), width)
+        dst = xh.at[c, :, span(k)] if own else stage.at[:, span(k)]
+        return pltpu.make_async_copy(x_ref.at[:, cols], dst, lsem.at[int(own), k])
+
+    barrier = pltpu.get_barrier_semaphore()
+    greeted = samp_peers + [peer for k, peer in enumerate(group, 1) if k != p]
+    for peer in greeted:
+        pl.semaphore_signal(barrier, inc=1, device_id=peer, device_id_type=MESH)
+
+    @pl.loop(0, CHUNKS)
+    def _(k):
+        load(k, False).start()
+        load(k, True).start()
+
+    taken_row, slot = iota((count, rows), 0), iota((count, rows), 1)
+    wide_row, wide_slot = iota((count, wide), 0), iota((count, wide), 1)
+    picks, wide_picks = jnp.zeros((count, rows), jnp.float32), jnp.zeros((count, wide), jnp.float32)
+    for j in range(count):
+        at = picks_ref[0, j]
+        picks = jnp.where((taken_row == j) & (slot == at), 1.0, picks)
+        wide_picks = jnp.where((wide_row == j) & (wide_slot == at + c * rows), 1.0, wide_picks)
+    probe[...] = jnp.concatenate([picks, jnp.ones_like(picks)], axis=0).astype(probe.dtype)
+    place = (iota((rows, wide), 0) + c * rows == iota((rows, wide), 1)).astype(jnp.float32)
+    aux[pl.ds(0, count), :] = exact(energy_ref[...], place)
+    aux[pl.ds(count, count), :] = wide_picks
+
+    def swap(k):
+        return remote(stage.at[:, span(k)], xh.at[c, :, span(k)], wsem.at[k], wrecv.at[k], pair)
+
+    def to_pair(k):
+        return remote(other.at[:, span(k)], rin.at[me, :, span(k)], psem.at[k], precv.at[k], pair)
+
+    def direct(k):
+        view = rin.at[duo(q), :, span(k)]
+        return [remote(view, view, osem.at[d, k], rsem.at[d, k], dev(near[d])) for d in range(2)]
+
+    def forward(k, d):
+        view = rin.at[duo(near[d]), :, span(k)]
+        return remote(view, view, fsem.at[k], drecv.at[k], dev(near[1 - d]))
+
+    def send(k):
+        view = rin.at[me + 1 - 2 * c, :, span(k)]
+        remote(view, view, psem.at[k], precv.at[k], pair).wait_recv()
+        for copy in direct(k):
+            copy.start()
+
+    def relay(k, d):
+        for e in range(2):
+            view = rin.at[duo(near[e]), :, span(k)]
+            remote(view, view, osem.at[e, k], rsem.at[e, k], pair).wait_recv()
+        forward(k, d).start()
+
+    def extract(k):
+        for own in (False, True):
+            load(k, own).wait()
+            step = min(width, 1024)
+
+            @pl.loop(0, width // step)
+            def _(s):
+                cols = pl.ds(pl.multiple_of(k * width + s * step, step), step)
+                block = xh[c, :, cols] if own else stage[:, cols]
+                taken = jnp.dot(probe[...], block, preferred_element_type=jnp.float32)
+                if own:
+                    rin[me, :, cols] = taken[:count].astype(rin.dtype)
+                    sums[c, :, cols] = taken[count:count + 1]
+                else:
+                    other[:, cols] = taken[:count].astype(other.dtype)
+                    sums[o, :, cols] = taken[count:count + 1]
+
+    extract(0)
+    pl.semaphore_wait(barrier, len(greeted))
+    to_pair(0).start()
+    auxes = [remote(aux, aux_all.at[me], asem.at[k], arecv.at[k], samp_peers[k]) for k in range(7)]
+
+    @pl.loop(1, EARLY + 1)
+    def _(k):
+        extract(k)
+        to_pair(k).start()
+        send(k - 1)
+
+    @pl.loop(EARLY + 1, CHUNKS)
+    def _(k):
+        extract(k)
+        to_pair(k).start()
+
+    first = remote(sums.at[o], sland.at[0], bsem.at[0], brecv.at[0], pair)
+    first.start()
+    for copy in auxes:
+        copy.start()
+    aux_all[me] = aux[...]
+
+    @pl.loop(0, CHUNKS)
+    def _(k):
+        swap(k).start()
+
+    first.wait_recv()
+    acc1[...] = sums[c] + sland[0]
+    part_of = [pl.ds(0, half // 2), pl.ds(half // 2, half // 2)]
+    second = [
+        remote(acc1.at[:, part_of[d]], sland.at[1, :, part_of[d]], bsem.at[1 + d], brecv.at[1 + d], dev(near[d]))
+        for d in range(2)
+    ]
+    for copy in second:
+        copy.start()
+    middle = (EARLY + AHEAD) // 2
+
+    @pl.loop(EARLY, middle)
+    def _(k):
+        send(k)
+
+    for copy in second:
+        copy.wait_recv()
+    acc2[...] = acc1[...] + sland[1]
+    third = [
+        remote(acc2.at[:, part_of[d]], sland.at[2, :, part_of[d]], bsem.at[3 + d], brecv.at[3 + d], dev(near[1 - d]))
+        for d in range(2)
+    ]
+    for copy in third:
+        copy.start()
+    relay(0, 0)
+
+    @pl.loop(middle, AHEAD)
+    def _(k):
+        send(k)
+
+    relay(1, 1)
+    for copy in third:
+        copy.wait_recv()
+    mean[...] = (acc2[...] + sland[2]) / total_rows
+    acc[...] = jnp.zeros_like(acc)
+
+    def process(k):
+        remote(stage.at[:, span(k)], xh.at[o, :, span(k)], wsem.at[k], wrecv.at[k], pair).wait_recv()
+        view = rin.at[duo(far), :, span(k)]
+        remote(view, view, fsem.at[k], drecv.at[k], pair).wait_recv()
+        step = min(width, 512)
+
+        @pl.loop(0, width // step)
+        def _(s):
+            cols = pl.ds(pl.multiple_of(k * width + s * step, step), step)
+            shift = mean[:, cols]
+            block = xh[:, :, cols].astype(jnp.float32).reshape(wide, step)
+            block = ((block - shift) * scale).astype(jnp.bfloat16)
+            xh[:, :, cols] = block.reshape(2, rows, step)
+            picked = rin[:, :, cols].astype(jnp.float32).reshape(8 * count, step)
+            picked = ((picked - shift) * scale).astype(jnp.bfloat16)
+            acc[...] += contract_last(picked, block)
+
+    @pl.loop(0, CHUNKS // 2)
+    def _(i):
+        for d in range(2):
+            k = 2 * i + d
+
+            @pl.when(k + AHEAD < CHUNKS)
+            def _():
+                send(k + AHEAD)
+
+            @pl.when(k + LAG < CHUNKS)
+            def _():
+                relay(k + LAG, d)
+
+            process(k)
+
+    rank = acc.shape[0]
+    own_rows = rank // 2
+    mine_rows = pl.ds(pl.multiple_of(c * own_rows, own_rows), own_rows)
+    their_rows = pl.ds(pl.multiple_of(o * own_rows, own_rows), own_rows)
+    give = remote(acc.at[their_rows], pland, tsem.at[0], trecv.at[0], pair)
+    give.start()
+    give.wait_recv()
+    mine[...] = acc[mine_rows, :] + pland[...]
+    across = [remote(mine, zland.at[z], tsem.at[k], trecv.at[k], par_peers[k - 1]) for k in range(1, p)]
+    for copy in across:
+        copy.start()
+    zland[z] = mine[...]
+    for k in range(7):
+        view = aux_all.at[lax.rem(me + 7 - k, 8)]
+        remote(view, view, asem.at[k], arecv.at[k], pair).wait_recv()
+    for k in range(1, p):
+        view = zland.at[lax.rem(z + p - k, p)]
+        remote(view, view, tsem.at[k], trecv.at[k], pair).wait_recv()
+    total = zland[0]
+    for j in range(1, p):
+        total = total + zland[j]
+    tot[...] = total
+    spot = lambda chip, core: sk.at[
+        pl.ds(pl.multiple_of(core * own_rows, own_rows), own_rows),
+        pl.ds(pl.multiple_of(chip * wide, wide), wide),
+    ]
+    here = pl.ds(pl.multiple_of(q * wide, wide), wide)
+    sk[mine_rows, here] = total
+    spread = [remote(tot, spot(q, c), tsem.at[p + k], trecv.at[p + k], samp_peers[k]) for k in range(7)]
+    for copy in spread:
+        copy.start()
+    vecs = count
+    lower = pl.ds(rank, vecs)
+    for chip in range(4):
+        cols = pl.ds(chip * wide, wide)
+        aug[lower, cols] = aux_all[2 * chip, :vecs, :] + aux_all[2 * chip + 1, :vecs, :]
+    energies = aug[lower, :]
+    big[...] = (iota(big.shape, 0) + rank == iota(big.shape, 1)).astype(jnp.float32)
+    for k in range(7):
+        source = lax.rem(me + 7 - k, 8)
+        view = spot(source // 2, lax.rem(source, 2))
+        remote(view, view, tsem.at[p + k], trecv.at[p + k], pair).wait_recv()
+
+    sketch = sk[...]
+    aug[pl.ds(0, rank), :] = sketch
+    for g in range(8):
+        cols = pl.ds((g // 2) * wide, wide)
+        line = pl.ds(g * vecs, vecs)
+        aug[line, cols] = aug[line, cols] + damping * aux_all[g, vecs:, :]
+    product = exact_t(aug[...], sketch)
+    big[:, pl.ds(0, rank)] = product[:rank]
+    inverse = eliminate(big[...], rank, 4)[:, rank:2 * rank]
+    dref[...] = (energies - exact(exact(product[rank:], inverse), sketch)) / damping
+
+    def small_inverse(matrix):
+        small[...] = (iota(small.shape, 0) + vecs == iota(small.shape, 1)).astype(jnp.float32)
+        small[:, pl.ds(0, vecs)] = matrix
+        return eliminate(small[...], vecs, 4)[:, vecs:2 * vecs]
+
+    quarter = half // 4
+    piece = quarter // 2
+    span2 = lambda chip, s: pl.ds(pl.multiple_of(chip * quarter + s * piece, piece), piece)
+    step = min(piece, 1024)
+    slot_of = z * 2 + c
+    sends = []
+
+    def begin(copy):
+        copy.start()
+        sends.append(copy)
+
+    def all_reduce(turn):
+        rounded = dref[:, here].astype(jnp.bfloat16)
+
+        def project(chip, s):
+            @pl.loop(0, piece // step)
+            def _(t):
+                cols = pl.ds(pl.multiple_of(chip * quarter + s * piece + t * step, step), step)
+                block = xh[:, :, cols].reshape(wide, step)
+                part[turn, :, cols] = jnp.dot(rounded, block, preferred_element_type=jnp.float32).astype(part.dtype)
+
+        halves = []
+        for j in range(2):
+            for d in range(2):
+                chip = near[d] if j else far
+                project(chip, d)
+                copy = remote(part.at[turn, :, span2(chip, d)], land1.at[turn, d, j], s1.at[turn, d, j],
+                              r1.at[turn, d, j], dev(near[d]))
+                halves.append(copy)
+                begin(copy)
+        for d in range(2):
+            project(near[1 - d], d)
+        later = []
+        for d in range(2):
+            halves[d].wait_recv()
+            mid[turn, d] = (
+                part[turn, :, span2(near[1 - d], d)].astype(jnp.float32) + land1[turn, d, 0].astype(jnp.float32)
+            ).astype(mid.dtype)
+            copy = remote(mid.at[turn, d], land2.at[turn, d], s2.at[turn, d], r2.at[turn, d], dev(near[1 - d]))
+            later.append(copy)
+            begin(copy)
+        for d in range(2):
+            project(q, d)
+        for d in range(2):
+            halves[2 + d].wait_recv()
+            keep[d] = part[turn, :, span2(q, d)].astype(jnp.float32) + land1[turn, d, 1].astype(jnp.float32)
+        for d in range(2):
+            later[d].wait_recv()
+            pf[c, turn, :, span2(q, d)] = (keep[d] + land2[turn, d].astype(jnp.float32)).astype(pf.dtype)
+            view = pf.at[c, turn, :, span2(q, d)]
+            begin(remote(view, view, s3.at[turn, d, d], r3.at[turn, d, d], dev(near[d])))
+        for d in range(2):
+            view = pf.at[c, turn, :, span2(q, 1 - d)]
+            begin(remote(view, view, s3.at[turn, d, 1 - d], r3.at[turn, d, 1 - d], dev(near[d])))
+        mine_cols = pl.ds(pl.multiple_of(q * quarter, quarter), quarter)
+        view = pf.at[c, turn, :, mine_cols]
+        begin(remote(view, view, s5.at[turn, 0], r5.at[turn, 0], pair))
+
+        sq[turn] = jnp.zeros(sq.shape[1:], jnp.float32)
+
+        @pl.loop(0, quarter // step)
+        def _(t):
+            block = pf[c, turn, :, pl.ds(pl.multiple_of(q * quarter + t * step, step), step)]
+            sq[turn, :, pl.ds(0, vecs)] += contract_last(block, block)
+
+        for k in range(1, 2 * p):
+            begin(remote(sq.at[turn], qland.at[turn, slot_of], s8.at[turn, k], r8.at[turn, k], group[k - 1]))
+        qland[turn, slot_of] = sq[turn]
+
+        def consume(chip):
+            @pl.loop(0, quarter // step)
+            def _(t):
+                cols = pl.ds(pl.multiple_of(chip * quarter + t * step, step), step)
+                msg[...] += contract_last(pf[c, turn, :, cols], xh[:, :, cols].reshape(wide, step))
+
+        if turn == 0:
+            msg[...] = jnp.zeros(msg.shape, jnp.float32)
+            consume(q)
+        for d in range(2):
+            view = pf.at[c, turn, :, span2(near[d], d)]
+            remote(view, view, s3.at[turn, d, d], r3.at[turn, d, d], pair).wait_recv()
+            begin(remote(view, view, s4.at[turn, d], r4.at[turn, d], dev(near[1 - d])))
+        for k in range(1, 2 * p):
+            there = lax.rem(z + p - lax.rem(k, p), p) * 2 + lax.rem(c + k // p, 2)
+            view = qland.at[turn, there]
+            remote(view, view, s8.at[turn, k], r8.at[turn, k], pair).wait_recv()
+        total = qland[turn, 0]
+        for j in range(1, 2 * p):
+            total = total + qland[turn, j]
+        qsum[turn] = total
+        qtot[turn, q] = total
+        for k, chip in enumerate(chips):
+            begin(remote(qsum.at[turn], qtot.at[turn, q], s9.at[turn, k], r9.at[turn, k], dev(chip)))
+        for d in range(2):
+            view = pf.at[c, turn, :, span2(near[d], 1 - d)]
+            remote(view, view, s3.at[turn, d, 1 - d], r3.at[turn, d, 1 - d], pair).wait_recv()
+            view = pf.at[c, turn, :, pl.ds(pl.multiple_of(near[d] * quarter, quarter), quarter)]
+            begin(remote(view, view, s5.at[turn, 1 + d], r5.at[turn, 1 + d], pair))
+            if turn == 0:
+                consume(near[d])
+        for d in range(2):
+            view = pf.at[c, turn, :, span2(far, d)]
+            remote(view, view, s4.at[turn, d], r4.at[turn, d], pair).wait_recv()
+            begin(remote(view, view, s5.at[turn, 3 + d], r5.at[turn, 3 + d], pair))
+        if turn == 0:
+            consume(far)
+            for k in range(1, 2 * p):
+                begin(remote(msg, mland.at[slot_of], s6.at[k], r6.at[k], group[k - 1]))
+            mland[slot_of] = msg[...]
+
+    def curve(turn, direction):
+        for k, chip in enumerate(chips):
+            view = qtot.at[turn, chip]
+            remote(view, view, s9.at[turn, k], r9.at[turn, k], pair).wait_recv()
+        total = qtot[turn, 0]
+        for j in range(1, 4):
+            total = total + qtot[turn, j]
+        return small_inverse(total[:, :vecs] + damping * exact_t(direction, direction))
+
+    all_reduce(0)
+    direction = dref[...]
+    gamma = exact_t(direction, energies)
+    alpha = exact(gamma, curve(0, direction))
+    gamma_inverse = small_inverse(gamma)
+    answer = exact(alpha, direction)
+    residual = energies - damping * answer
+    for k in range(1, 2 * p):
+        there = lax.rem(z + p - lax.rem(k, p), p) * 2 + lax.rem(c + k // p, 2)
+        view = mland.at[there]
+        remote(view, view, s6.at[k], r6.at[k], pair).wait_recv()
+    total = mland[0]
+    for j in range(1, 2 * p):
+        total = total + mland[j]
+    img[:, here] = total
+    rres[...] = total
+    for k, chip in enumerate(chips):
+        begin(remote(rres, img.at[:, here], s7.at[k], r7.at[k], dev(chip)))
+    for k, chip in enumerate(chips):
+        view = img.at[:, pl.ds(pl.multiple_of(chip * wide, wide), wide)]
+        remote(view, view, s7.at[k], r7.at[k], pair).wait_recv()
+    residual = residual - exact(alpha, img[...])
+    fresh = (residual - exact(exact(exact_t(residual, sketch), inverse), sketch)) / damping
+    gamma_next = exact_t(fresh, residual)
+    dref[...] = fresh + exact(exact(gamma_next, gamma_inverse), direction)
+    all_reduce(1)
+    direction = dref[...]
+    alpha_next = exact(gamma_next, curve(1, direction))
+    dref[...] = answer + exact(alpha_next, direction)
+    sol_ref[...] = dref[:, here]
+    alpha_ref[0] = alpha
+    alpha_ref[1] = alpha_next
+    out = pltpu.make_async_copy(pf.at[c], pf_ref.at[c], lsem.at[0, 0])
+    out.start()
+    for turn in range(2):
+        for k, chip in enumerate([q, near[0], near[1]]):
+            view = pf.at[o, turn, :, pl.ds(pl.multiple_of(chip * quarter, quarter), quarter)]
+            remote(view, view, s5.at[turn, k], r5.at[turn, k], pair).wait_recv()
+        for d in range(2):
+            view = pf.at[o, turn, :, span2(far, d)]
+            remote(view, view, s5.at[turn, 3 + d], r5.at[turn, 3 + d], pair).wait_recv()
+    out_two = pltpu.make_async_copy(pf.at[o], pf_ref.at[o], lsem.at[1, 0])
+    out_two.start()
+
+    @pl.loop(0, CHUNKS // 2)
+    def _(i):
+        for d in range(2):
+            k = 2 * i + d
+            swap(k).wait_send()
+            to_pair(k).wait_send()
+            for copy in direct(k):
+                copy.wait_send()
+            forward(k, d).wait_send()
+
+    for copy in auxes + [first] + second + third + [give] + across + spread + sends:
+        copy.wait_send()
+    out.wait()
+    out_two.wait()
+
+
+def main_call(x, energies, picks, p, total_rows, scale, ident):
+    rows, full = x.shape
+    half = full // 2
+    vecs, count = energies.shape[0], picks.shape[1]
+    rank, wide = 8 * count, 2 * rows
+    total = 4 * wide
+    piece = half // 8
+    bf, f32 = jnp.bfloat16, jnp.float32
+    vmem, hbm = pl.BlockSpec(memory_space=pltpu.VMEM), pl.BlockSpec(memory_space=pl.ANY)
+    smem = pl.BlockSpec(memory_space=pltpu.SMEM)
+    dma = lambda *shape: pltpu.SemaphoreType.DMA(shape)
+    buf = lambda kind, *shape: pltpu.VMEM(shape, kind)
+    return pl.pallas_call(
+        functools.partial(main_kernel, p, total_rows, scale),
+        out_shape=(
+            jax.ShapeDtypeStruct((2, 2, vecs, half), bf),
+            jax.ShapeDtypeStruct((2, vecs, vecs), f32),
+            jax.ShapeDtypeStruct((vecs, wide), f32),
+        ),
+        in_specs=[hbm, vmem, smem],
+        out_specs=(hbm, vmem, vmem),
+        scratch_shapes=[
+            buf(bf, rows, half), buf(bf, 2, rows, half), buf(bf, count, half), buf(bf, 8, count, half),
+            buf(bf, 2 * count, rows), buf(f32, 2 * count, wide), buf(f32, 8, 2 * count, wide),
+            buf(f32, 2, 1, half), buf(f32, 3, 1, half), buf(f32, 1, half), buf(f32, 1, half), buf(f32, 1, half),
+            buf(f32, rank, wide), buf(f32, rank // 2, wide), buf(f32, rank // 2, wide),
+            buf(f32, p, rank // 2, wide), buf(f32, rank // 2, wide), buf(f32, rank, total),
+            buf(f32, rank + vecs, total), buf(f32, rank, 2 * rank), buf(f32, vecs, 128), buf(f32, vecs, total),
+            buf(f32, vecs, wide), buf(bf, 2, vecs, half), buf(bf, 2, 2, 2, vecs, piece), buf(bf, 2, 2, vecs, piece),
+            buf(f32, 2, vecs, piece), buf(bf, 2, 2, vecs, piece), buf(bf, 2, 2, vecs, half),
+            buf(f32, 2, vecs, 128), buf(f32, 2, 2 * p, vecs, 128), buf(f32, 2, vecs, 128),
+            buf(f32, 2, 4, vecs, 128), buf(f32, vecs, wide), buf(f32, 2 * p, vecs, wide), buf(f32, vecs, total),
+            dma(2, CHUNKS), dma(CHUNKS), dma(CHUNKS), dma(CHUNKS), dma(CHUNKS), dma(2, CHUNKS), dma(2, CHUNKS),
+            dma(CHUNKS), dma(CHUNKS), dma(5), dma(5), dma(7), dma(7), dma(p + 7), dma(p + 7),
+            dma(2, 2, 2), dma(2, 2, 2), dma(2, 2), dma(2, 2), dma(2, 2, 2), dma(2, 2, 2), dma(2, 2), dma(2, 2),
+            dma(2, 5), dma(2, 5), dma(2 * p), dma(2 * p), dma(3), dma(3), dma(2, 2 * p), dma(2, 2 * p),
+            dma(2, 3), dma(2, 3),
+        ],
+        compiler_params=pltpu.CompilerParams(
+            collective_id=ident, has_side_effects=True, vmem_limit_bytes=60 * 2**20
+        ),
+    )(x, energies, picks)
+
+
+def finish_kernel(pf_ref, alpha_ref, sol_ref, update_ref, out_ref):
+    vecs, rows = out_ref.shape
+    weights = jnp.concatenate([alpha_ref[0], alpha_ref[1]], axis=1)
+    upper = weights.astype(jnp.bfloat16)
+    lower = (weights - upper.astype(jnp.float32)).astype(jnp.bfloat16)
+    both = jnp.concatenate([upper.astype(jnp.float32), lower.astype(jnp.float32)], axis=0).astype(jnp.bfloat16)
+    step = 1024
+    for t in range(update_ref.shape[1] // step):
+        cols = pl.ds(t * step, step)
+        block = pf_ref[0, :, :, cols].astype(jnp.float32).reshape(2 * vecs, step).astype(jnp.bfloat16)
+        out = jnp.dot(both, block, preferred_element_type=jnp.float32)
+        update_ref[:, cols] = out[:vecs] + out[vecs:]
+    core = lax.rem(lax.axis_index("samp"), 2)
+    out_ref[...] = jnp.where(core == 0, sol_ref[:, :rows], sol_ref[:, rows:])
+
+
+def finish_call(pf, alpha, sol):
+    _, _, vecs, half = pf.shape
+    block = half // 4
+    whole = lambda shape: pl.BlockSpec(shape, lambda i: (0,) * len(shape))
+    return pl.pallas_call(
+        finish_kernel,
+        grid=(2 * half // block,),
+        out_shape=(
+            jax.ShapeDtypeStruct((vecs, 2 * half), jnp.float32),
+            jax.ShapeDtypeStruct((vecs, sol.shape[1] // 2), jnp.float32),
+        ),
+        in_specs=[
+            pl.BlockSpec((1, 2, vecs, block), lambda i: (i // 4, 0, 0, i % 4)), whole(alpha.shape), whole(sol.shape)
+        ],
+        out_specs=(pl.BlockSpec((vecs, block), lambda i: (0, i)), whole((vecs, sol.shape[1] // 2))),
+    )(pf, alpha, sol)
+
+
+def paired_body(log_derivs, energies, nys_rows):
+    rows, width = log_derivs.shape
+    n, p = lax.axis_size("samp"), lax.axis_size("par")
+    pf, alpha, answer = main_call(log_derivs, energies.T, nys_rows, p, n * rows, 1.0 / math.sqrt(width * p), 0)
+    update, own = finish_call(pf, alpha, answer)
+    return (update.T, own.T)
+
+
 def solution(mesh):
+    n = mesh.shape["samp"]
+
+    def body(log_derivs, energies, nys_rows):
+        rows, count = log_derivs.shape[0], energies.shape[1]
+        paired = n == 8 and rows == 64 and count == 8 and nys_rows.shape[1] == count
+        return (paired_body if paired else general_body)(log_derivs, energies, nys_rows)
+
     return jax.shard_map(
         body,
         mesh=mesh,

time: 213 us -> 117 us (0.55)
  matrix products: 44.6 us -> 0 us
  Pallas kernels: 146 us -> 116 us
  other arithmetic: 15.5 us -> 0 us
  local copies, waits for them, and re-layouts: 4.92 us -> 0 us
    dot_general x21 -> x0, matrix products: 44 us -> none  [the longest x15 16.9 us: hdot(): return jnp.dot(left, right, precision=lax.Precision.HIGHEST)]
    pallas_call x9 -> x2, Pallas kernels: 146 us -> 116 us  [the longest x1 110 us: main_call(): pl.pallas_call(functools.partial(main_kernel, p, total_rows, scale), out_...]
    another operation x5 -> x0, other arithmetic: 12.1 us -> none  [the longest x3 6.52 us: body(): factor = jnp.linalg.cholesky(damping * core_block + hdot(sketch.T, sketch))]
where the time goes in v2:
time: 117 us
  Pallas kernels  116 us (99%)
    pallas_call x1, Pallas kernels, main_call(): pl.pallas_call(functools.partial(main_kernel, p, total_rows, scale), out_...  110 us
    pallas_call x1, Pallas kernels, finish_call(): pl.pallas_call(finish_kernel, grid=(2 * half // block,), out_shape=(jax.S...  6.59 us

profile of v2, /device:TPU:0, one launch (start us, length us, event | category | flops | bytes accessed | tf_op | source)
XLA Modules:
  0.0 117.1 jit_solution(15414357864398481032)
XLA Ops:
  0.6 109.8 %shard_map.50 = (bf16[2,2,8,32768]{3,2,1,0:T(8,128)(2,1)}, f32[2,8,8]{2,1,0:T(8,128)}, f32[8,128]{1,0:T(8,128)}) custom-call(bf16[64,65536]{1,0:T(8,128)(2,1)} %x_ref.1, f32[8,64]{1,0:T(8,128)} %bitcast.3, s32[1,8]{1,0:T(1,128)} %picks_ref.1), custom_call_target="tpu_custom_call" | custom-call | tf_op jit(solution)/shard_map/pallas_call | solution.py:915
  110.5 6.6 %shard_map.51 = (f32[8,65536]{1,0:T(8,128)}, f32[8,64]{1,0:T(8,128)}) custom-call(bf16[2,2,8,32768]{3,2,1,0:T(8,128)(2,1)} %get-tuple-element.7.pf_ref, f32[2,8,8]{2,1,0:T(8,128)} %get-tuple-element.8.alpha_ref, f32[8,128]{1,0:T(8,128)} %get-tuple-element.9.sol_ref), custom_call_target="tpu_custom_call" | custom-call | tf_op jit(solution)/shard_map/pallas_call | solution.py:967

commit v3 on v2

--- a/solution.py
+++ b/solution.py
@@ -419,9 +419,10 @@
 
 
 CHUNKS = 8
-EARLY = 2
-AHEAD = 4
+EARLY = 3
+AHEAD = 5
 LAG = 2
+FINISH = 1
 
 
 def contract_last(left, right, precision=None):
@@ -474,9 +475,9 @@
     return matrix
 
 
-def main_kernel(p, total_rows, scale, x_ref, energy_ref, picks_ref, pf_ref, alpha_ref, sol_ref,
+def main_kernel(p, total_rows, scale, x_ref, energy_ref, picks_ref, pf, alpha_ref, sol_ref,
                 stage, xh, other, rin, probe, aux, aux_all, sums, sland, acc1, acc2, mean, acc, pland, mine, zland,
-                tot, sk, aug, big, small, dref, rres, part, land1, mid, keep, land2, pf, sq, qland, qsum, qtot,
+                tot, sk, aug, big, small, dref, rres, part, land1, mid, keep, land2, sq, qland, qsum, qtot,
                 msg, mland, img,
                 lsem, wsem, wrecv, psem, precv, osem, rsem, fsem, drecv, bsem, brecv, asem, arecv, tsem, trecv,
                 s1, r1, s2, r2, s3, r3, s4, r4, s5, r5, s6, r6, s7, r7, s8, r8, s9, r9):
@@ -521,9 +522,6 @@
         picks = jnp.where((taken_row == j) & (slot == at), 1.0, picks)
         wide_picks = jnp.where((wide_row == j) & (wide_slot == at + c * rows), 1.0, wide_picks)
     probe[...] = jnp.concatenate([picks, jnp.ones_like(picks)], axis=0).astype(probe.dtype)
-    place = (iota((rows, wide), 0) + c * rows == iota((rows, wide), 1)).astype(jnp.float32)
-    aux[pl.ds(0, count), :] = exact(energy_ref[...], place)
-    aux[pl.ds(count, count), :] = wide_picks
 
     def swap(k):
         return remote(stage.at[:, span(k)], xh.at[c, :, span(k)], wsem.at[k], wrecv.at[k], pair)
@@ -552,21 +550,19 @@
         forward(k, d).start()
 
     def extract(k):
-        for own in (False, True):
-            load(k, own).wait()
-            step = min(width, 1024)
-
-            @pl.loop(0, width // step)
-            def _(s):
-                cols = pl.ds(pl.multiple_of(k * width + s * step, step), step)
-                block = xh[c, :, cols] if own else stage[:, cols]
-                taken = jnp.dot(probe[...], block, preferred_element_type=jnp.float32)
-                if own:
-                    rin[me, :, cols] = taken[:count].astype(rin.dtype)
-                    sums[c, :, cols] = taken[count:count + 1]
-                else:
-                    other[:, cols] = taken[:count].astype(other.dtype)
-                    sums[o, :, cols] = taken[count:count + 1]
+        load(k, False).wait()
+        load(k, True).wait()
+        step = min(width, 2048)
+
+        @pl.loop(0, width // step)
+        def _(s):
+            cols = pl.ds(pl.multiple_of(k * width + s * step, step), step)
+            theirs = jnp.dot(probe[...], stage[:, cols], preferred_element_type=jnp.float32)
+            other[:, cols] = theirs[:count].astype(other.dtype)
+            sums[o, :, cols] = theirs[count:count + 1]
+            ours = jnp.dot(probe[...], xh[c, :, cols], preferred_element_type=jnp.float32)
+            rin[me, :, cols] = ours[:count].astype(rin.dtype)
+            sums[c, :, cols] = ours[count:count + 1]
 
     extract(0)
     pl.semaphore_wait(barrier, len(greeted))
@@ -586,13 +582,17 @@
 
     first = remote(sums.at[o], sland.at[0], bsem.at[0], brecv.at[0], pair)
     first.start()
-    for copy in auxes:
-        copy.start()
-    aux_all[me] = aux[...]
 
     @pl.loop(0, CHUNKS)
     def _(k):
         swap(k).start()
+
+    place = (iota((rows, wide), 0) + c * rows == iota((rows, wide), 1)).astype(jnp.float32)
+    aux[pl.ds(0, count), :] = exact(energy_ref[...], place)
+    aux[pl.ds(count, count), :] = wide_picks
+    for copy in auxes:
+        copy.start()
+    aux_all[me] = aux[...]
 
     first.wait_recv()
     acc1[...] = sums[c] + sland[0]
@@ -693,6 +693,16 @@
     spread = [remote(tot, spot(q, c), tsem.at[p + k], trecv.at[p + k], samp_peers[k]) for k in range(7)]
     for copy in spread:
         copy.start()
+    @pl.loop(0, CHUNKS // 2)
+    def _(i):
+        for d in range(2):
+            k = 2 * i + d
+            swap(k).wait_send()
+            to_pair(k).wait_send()
+            for copy in direct(k):
+                copy.wait_send()
+            forward(k, d).wait_send()
+
     vecs = count
     lower = pl.ds(rank, vecs)
     for chip in range(4):
@@ -724,7 +734,11 @@
     quarter = half // 4
     piece = quarter // 2
     span2 = lambda chip, s: pl.ds(pl.multiple_of(chip * quarter + s * piece, piece), piece)
-    step = min(piece, 1024)
+    small_piece = piece // 2
+    span3 = lambda chip, s, u: pl.ds(
+        pl.multiple_of(chip * quarter + s * piece + u * small_piece, small_piece), small_piece
+    )
+    step = min(small_piece, 1024)
     slot_of = z * 2 + c
     sends = []
 
@@ -732,58 +746,69 @@
         copy.start()
         sends.append(copy)
 
-    def all_reduce(turn):
+    def all_reduce(turn, idle):
         rounded = dref[:, here].astype(jnp.bfloat16)
 
-        def project(chip, s):
-            @pl.loop(0, piece // step)
-            def _(t):
-                cols = pl.ds(pl.multiple_of(chip * quarter + s * piece + t * step, step), step)
+        def project(chip, s, u):
+            for t in range(small_piece // step):
+                cols = pl.ds(pl.multiple_of(chip * quarter + s * piece + u * small_piece + t * step, step), step)
                 block = xh[:, :, cols].reshape(wide, step)
                 part[turn, :, cols] = jnp.dot(rounded, block, preferred_element_type=jnp.float32).astype(part.dtype)
 
-        halves = []
+        first_hop, second_hop = {}, {}
         for j in range(2):
+            for u in range(2):
+                for d in range(2):
+                    chip = near[d] if j else far
+                    project(chip, d, u)
+                    copy = remote(part.at[turn, :, span3(chip, d, u)], land1.at[turn, d, j, u],
+                                  s1.at[turn, d, j, u], r1.at[turn, d, j, u], dev(near[d]))
+                    first_hop[j, u, d] = copy
+                    begin(copy)
+        for u in range(2):
             for d in range(2):
-                chip = near[d] if j else far
-                project(chip, d)
-                copy = remote(part.at[turn, :, span2(chip, d)], land1.at[turn, d, j], s1.at[turn, d, j],
-                              r1.at[turn, d, j], dev(near[d]))
-                halves.append(copy)
+                project(near[1 - d], d, u)
+        for u in range(2):
+            for d in range(2):
+                first_hop[0, u, d].wait_recv()
+                mid[turn, d, u] = (
+                    part[turn, :, span3(near[1 - d], d, u)].astype(jnp.float32)
+                    + land1[turn, d, 0, u].astype(jnp.float32)
+                ).astype(mid.dtype)
+                copy = remote(mid.at[turn, d, u], land2.at[turn, d, u], s2.at[turn, d, u], r2.at[turn, d, u],
+                              dev(near[1 - d]))
+                second_hop[u, d] = copy
                 begin(copy)
-        for d in range(2):
-            project(near[1 - d], d)
-        later = []
-        for d in range(2):
-            halves[d].wait_recv()
-            mid[turn, d] = (
-                part[turn, :, span2(near[1 - d], d)].astype(jnp.float32) + land1[turn, d, 0].astype(jnp.float32)
-            ).astype(mid.dtype)
-            copy = remote(mid.at[turn, d], land2.at[turn, d], s2.at[turn, d], r2.at[turn, d], dev(near[1 - d]))
-            later.append(copy)
-            begin(copy)
-        for d in range(2):
-            project(q, d)
-        for d in range(2):
-            halves[2 + d].wait_recv()
-            keep[d] = part[turn, :, span2(q, d)].astype(jnp.float32) + land1[turn, d, 1].astype(jnp.float32)
-        for d in range(2):
-            later[d].wait_recv()
-            pf[c, turn, :, span2(q, d)] = (keep[d] + land2[turn, d].astype(jnp.float32)).astype(pf.dtype)
-            view = pf.at[c, turn, :, span2(q, d)]
-            begin(remote(view, view, s3.at[turn, d, d], r3.at[turn, d, d], dev(near[d])))
-        for d in range(2):
-            view = pf.at[c, turn, :, span2(q, 1 - d)]
-            begin(remote(view, view, s3.at[turn, d, 1 - d], r3.at[turn, d, 1 - d], dev(near[d])))
+        for u in range(2):
+            for d in range(2):
+                project(q, d, u)
+        idle()
+        for u in range(2):
+            for d in range(2):
+                first_hop[1, u, d].wait_recv()
+                keep[d, u] = (
+                    part[turn, :, span3(q, d, u)].astype(jnp.float32) + land1[turn, d, 1, u].astype(jnp.float32)
+                )
+        for u in range(2):
+            for d in range(2):
+                second_hop[u, d].wait_recv()
+                pf[c, pl.ds(turn * vecs, vecs), span3(q, d, u)] = (
+                    keep[d, u] + land2[turn, d, u].astype(jnp.float32)
+                ).astype(pf.dtype)
+                view = pf.at[c, pl.ds(turn * vecs, vecs), span3(q, d, u)]
+                begin(remote(view, view, s3.at[turn, d, d, u], r3.at[turn, d, d, u], dev(near[d])))
+            for d in range(2):
+                view = pf.at[c, pl.ds(turn * vecs, vecs), span3(q, 1 - d, u)]
+                begin(remote(view, view, s3.at[turn, d, 1 - d, u], r3.at[turn, d, 1 - d, u], dev(near[d])))
         mine_cols = pl.ds(pl.multiple_of(q * quarter, quarter), quarter)
-        view = pf.at[c, turn, :, mine_cols]
+        view = pf.at[c, pl.ds(turn * vecs, vecs), mine_cols]
         begin(remote(view, view, s5.at[turn, 0], r5.at[turn, 0], pair))
 
         sq[turn] = jnp.zeros(sq.shape[1:], jnp.float32)
 
         @pl.loop(0, quarter // step)
         def _(t):
-            block = pf[c, turn, :, pl.ds(pl.multiple_of(q * quarter + t * step, step), step)]
+            block = pf[c, pl.ds(turn * vecs, vecs), pl.ds(pl.multiple_of(q * quarter + t * step, step), step)]
             sq[turn, :, pl.ds(0, vecs)] += contract_last(block, block)
 
         for k in range(1, 2 * p):
@@ -794,15 +819,16 @@
             @pl.loop(0, quarter // step)
             def _(t):
                 cols = pl.ds(pl.multiple_of(chip * quarter + t * step, step), step)
-                msg[...] += contract_last(pf[c, turn, :, cols], xh[:, :, cols].reshape(wide, step))
+                msg[...] += contract_last(pf[c, pl.ds(turn * vecs, vecs), cols], xh[:, :, cols].reshape(wide, step))
 
         if turn == 0:
             msg[...] = jnp.zeros(msg.shape, jnp.float32)
             consume(q)
-        for d in range(2):
-            view = pf.at[c, turn, :, span2(near[d], d)]
-            remote(view, view, s3.at[turn, d, d], r3.at[turn, d, d], pair).wait_recv()
-            begin(remote(view, view, s4.at[turn, d], r4.at[turn, d], dev(near[1 - d])))
+        for u in range(2):
+            for d in range(2):
+                view = pf.at[c, pl.ds(turn * vecs, vecs), span3(near[d], d, u)]
+                remote(view, view, s3.at[turn, d, d, u], r3.at[turn, d, d, u], pair).wait_recv()
+                begin(remote(view, view, s4.at[turn, d, u], r4.at[turn, d, u], dev(near[1 - d])))
         for k in range(1, 2 * p):
             there = lax.rem(z + p - lax.rem(k, p), p) * 2 + lax.rem(c + k // p, 2)
             view = qland.at[turn, there]
@@ -815,15 +841,18 @@
         for k, chip in enumerate(chips):
             begin(remote(qsum.at[turn], qtot.at[turn, q], s9.at[turn, k], r9.at[turn, k], dev(chip)))
         for d in range(2):
-            view = pf.at[c, turn, :, span2(near[d], 1 - d)]
-            remote(view, view, s3.at[turn, d, 1 - d], r3.at[turn, d, 1 - d], pair).wait_recv()
-            view = pf.at[c, turn, :, pl.ds(pl.multiple_of(near[d] * quarter, quarter), quarter)]
+            for u in range(2):
+                view = pf.at[c, pl.ds(turn * vecs, vecs), span3(near[d], 1 - d, u)]
+                remote(view, view, s3.at[turn, d, 1 - d, u], r3.at[turn, d, 1 - d, u], pair).wait_recv()
+            view = pf.at[c, pl.ds(turn * vecs, vecs), pl.ds(pl.multiple_of(near[d] * quarter, quarter), quarter)]
             begin(remote(view, view, s5.at[turn, 1 + d], r5.at[turn, 1 + d], pair))
             if turn == 0:
                 consume(near[d])
         for d in range(2):
-            view = pf.at[c, turn, :, span2(far, d)]
-            remote(view, view, s4.at[turn, d], r4.at[turn, d], pair).wait_recv()
+            for u in range(2):
+                view = pf.at[c, pl.ds(turn * vecs, vecs), span3(far, d, u)]
+                remote(view, view, s4.at[turn, d, u], r4.at[turn, d, u], pair).wait_recv()
+            view = pf.at[c, pl.ds(turn * vecs, vecs), span2(far, d)]
             begin(remote(view, view, s5.at[turn, 3 + d], r5.at[turn, 3 + d], pair))
         if turn == 0:
             consume(far)
@@ -840,7 +869,11 @@
             total = total + qtot[turn, j]
         return small_inverse(total[:, :vecs] + damping * exact_t(direction, direction))
 
-    all_reduce(0)
+    def settle(copies):
+        for copy in copies:
+            copy.wait_send()
+
+    all_reduce(0, lambda: settle(auxes + [first] + second + third + [give] + across + spread))
     direction = dref[...]
     gamma = exact_t(direction, energies)
     alpha = exact(gamma, curve(0, direction))
@@ -865,39 +898,24 @@
     fresh = (residual - exact(exact(exact_t(residual, sketch), inverse), sketch)) / damping
     gamma_next = exact_t(fresh, residual)
     dref[...] = fresh + exact(exact(gamma_next, gamma_inverse), direction)
-    all_reduce(1)
+    settled = len(sends)
+    all_reduce(1, lambda: settle(sends[:settled]))
     direction = dref[...]
     alpha_next = exact(gamma_next, curve(1, direction))
     dref[...] = answer + exact(alpha_next, direction)
     sol_ref[...] = dref[:, here]
     alpha_ref[0] = alpha
     alpha_ref[1] = alpha_next
-    out = pltpu.make_async_copy(pf.at[c], pf_ref.at[c], lsem.at[0, 0])
-    out.start()
     for turn in range(2):
         for k, chip in enumerate([q, near[0], near[1]]):
-            view = pf.at[o, turn, :, pl.ds(pl.multiple_of(chip * quarter, quarter), quarter)]
+            view = pf.at[o, pl.ds(turn * vecs, vecs), pl.ds(pl.multiple_of(chip * quarter, quarter), quarter)]
             remote(view, view, s5.at[turn, k], r5.at[turn, k], pair).wait_recv()
         for d in range(2):
-            view = pf.at[o, turn, :, span2(far, d)]
+            view = pf.at[o, pl.ds(turn * vecs, vecs), span2(far, d)]
             remote(view, view, s5.at[turn, 3 + d], r5.at[turn, 3 + d], pair).wait_recv()
-    out_two = pltpu.make_async_copy(pf.at[o], pf_ref.at[o], lsem.at[1, 0])
-    out_two.start()
-
-    @pl.loop(0, CHUNKS // 2)
-    def _(i):
-        for d in range(2):
-            k = 2 * i + d
-            swap(k).wait_send()
-            to_pair(k).wait_send()
-            for copy in direct(k):
-                copy.wait_send()
-            forward(k, d).wait_send()
-
-    for copy in auxes + [first] + second + third + [give] + across + spread + sends:
+
+    for copy in sends[settled:]:
         copy.wait_send()
-    out.wait()
-    out_two.wait()
 
 
 def main_call(x, energies, picks, p, total_rows, scale, ident):
@@ -908,19 +926,19 @@
     total = 4 * wide
     piece = half // 8
     bf, f32 = jnp.bfloat16, jnp.float32
-    vmem, hbm = pl.BlockSpec(memory_space=pltpu.VMEM), pl.BlockSpec(memory_space=pl.ANY)
+    vmem, hbm = pl.BlockSpec(memory_space=pltpu.VMEM), pl.BlockSpec(memory_space=pltpu.HBM)
     smem = pl.BlockSpec(memory_space=pltpu.SMEM)
     dma = lambda *shape: pltpu.SemaphoreType.DMA(shape)
     buf = lambda kind, *shape: pltpu.VMEM(shape, kind)
     return pl.pallas_call(
         functools.partial(main_kernel, p, total_rows, scale),
         out_shape=(
-            jax.ShapeDtypeStruct((2, 2, vecs, half), bf),
+            jax.ShapeDtypeStruct((2, 2 * vecs, half), bf),
             jax.ShapeDtypeStruct((2, vecs, vecs), f32),
             jax.ShapeDtypeStruct((vecs, wide), f32),
         ),
         in_specs=[hbm, vmem, smem],
-        out_specs=(hbm, vmem, vmem),
+        out_specs=(vmem, vmem, vmem),
         scratch_shapes=[
             buf(bf, rows, half), buf(bf, 2, rows, half), buf(bf, count, half), buf(bf, 8, count, half),
             buf(bf, 2 * count, rows), buf(f32, 2 * count, wide), buf(f32, 8, 2 * count, wide),
@@ -928,18 +946,19 @@
             buf(f32, rank, wide), buf(f32, rank // 2, wide), buf(f32, rank // 2, wide),
             buf(f32, p, rank // 2, wide), buf(f32, rank // 2, wide), buf(f32, rank, total),
             buf(f32, rank + vecs, total), buf(f32, rank, 2 * rank), buf(f32, vecs, 128), buf(f32, vecs, total),
-            buf(f32, vecs, wide), buf(bf, 2, vecs, half), buf(bf, 2, 2, 2, vecs, piece), buf(bf, 2, 2, vecs, piece),
-            buf(f32, 2, vecs, piece), buf(bf, 2, 2, vecs, piece), buf(bf, 2, 2, vecs, half),
+            buf(f32, vecs, wide), buf(bf, 2, vecs, half), buf(bf, 2, 2, 2, 2, vecs, piece // 2), buf(bf, 2, 2, 2, vecs, piece // 2),
+            buf(f32, 2, 2, vecs, piece // 2), buf(bf, 2, 2, 2, vecs, piece // 2),
             buf(f32, 2, vecs, 128), buf(f32, 2, 2 * p, vecs, 128), buf(f32, 2, vecs, 128),
             buf(f32, 2, 4, vecs, 128), buf(f32, vecs, wide), buf(f32, 2 * p, vecs, wide), buf(f32, vecs, total),
             dma(2, CHUNKS), dma(CHUNKS), dma(CHUNKS), dma(CHUNKS), dma(CHUNKS), dma(2, CHUNKS), dma(2, CHUNKS),
             dma(CHUNKS), dma(CHUNKS), dma(5), dma(5), dma(7), dma(7), dma(p + 7), dma(p + 7),
-            dma(2, 2, 2), dma(2, 2, 2), dma(2, 2), dma(2, 2), dma(2, 2, 2), dma(2, 2, 2), dma(2, 2), dma(2, 2),
+            dma(2, 2, 2, 2), dma(2, 2, 2, 2), dma(2, 2, 2), dma(2, 2, 2), dma(2, 2, 2, 2), dma(2, 2, 2, 2),
+            dma(2, 2, 2), dma(2, 2, 2),
             dma(2, 5), dma(2, 5), dma(2 * p), dma(2 * p), dma(3), dma(3), dma(2, 2 * p), dma(2, 2 * p),
             dma(2, 3), dma(2, 3),
         ],
         compiler_params=pltpu.CompilerParams(
-            collective_id=ident, has_side_effects=True, vmem_limit_bytes=60 * 2**20
+            collective_id=ident, has_side_effects=True, vmem_limit_bytes=48 * 2**20
         ),
     )(x, energies, picks)
 
@@ -950,31 +969,31 @@
     upper = weights.astype(jnp.bfloat16)
     lower = (weights - upper.astype(jnp.float32)).astype(jnp.bfloat16)
     both = jnp.concatenate([upper.astype(jnp.float32), lower.astype(jnp.float32)], axis=0).astype(jnp.bfloat16)
-    step = 1024
-    for t in range(update_ref.shape[1] // step):
-        cols = pl.ds(t * step, step)
-        block = pf_ref[0, :, :, cols].astype(jnp.float32).reshape(2 * vecs, step).astype(jnp.bfloat16)
-        out = jnp.dot(both, block, preferred_element_type=jnp.float32)
-        update_ref[:, cols] = out[:vecs] + out[vecs:]
+    width = update_ref.shape[1]
+    per_core = pf_ref.shape[2] // width
+    i = pl.program_id(0)
+    step = min(width, 1024)
+    for t in range(width // step):
+        cols = pl.ds(pl.multiple_of(lax.rem(i, per_core) * width + t * step, step), step)
+        out = jnp.dot(both, pf_ref[i // per_core, :, cols], preferred_element_type=jnp.float32)
+        update_ref[:, pl.ds(t * step, step)] = out[:vecs] + out[vecs:]
     core = lax.rem(lax.axis_index("samp"), 2)
     out_ref[...] = jnp.where(core == 0, sol_ref[:, :rows], sol_ref[:, rows:])
 
 
 def finish_call(pf, alpha, sol):
-    _, _, vecs, half = pf.shape
-    block = half // 4
-    whole = lambda shape: pl.BlockSpec(shape, lambda i: (0,) * len(shape))
+    _, vecs, half = pf.shape
+    vecs = vecs // 2
+    block = half // FINISH
+    vmem = pl.BlockSpec(memory_space=pltpu.VMEM)
+    own = (vecs, sol.shape[1] // 2)
     return pl.pallas_call(
         finish_kernel,
         grid=(2 * half // block,),
-        out_shape=(
-            jax.ShapeDtypeStruct((vecs, 2 * half), jnp.float32),
-            jax.ShapeDtypeStruct((vecs, sol.shape[1] // 2), jnp.float32),
-        ),
-        in_specs=[
-            pl.BlockSpec((1, 2, vecs, block), lambda i: (i // 4, 0, 0, i % 4)), whole(alpha.shape), whole(sol.shape)
-        ],
-        out_specs=(pl.BlockSpec((vecs, block), lambda i: (0, i)), whole((vecs, sol.shape[1] // 2))),
+        out_shape=(jax.ShapeDtypeStruct((vecs, 2 * half), jnp.float32), jax.ShapeDtypeStruct(own, jnp.float32)),
+        in_specs=[vmem, vmem, vmem],
+        out_specs=(pl.BlockSpec((vecs, block), lambda i: (0, i)), pl.BlockSpec(own, lambda i: (0, 0))),
+        compiler_params=pltpu.CompilerParams(vmem_limit_bytes=8 * 2**20),
     )(pf, alpha, sol)
 
 

time: 117 us -> 110 us (0.940)
  Pallas kernels: 116 us -> 108 us
  local copies, waits for them, and re-layouts: 0 us -> 1.33 us
    pallas_call x1, Pallas kernels: 6.59 us -> 1.95 us  [finish_call(): pl.pallas_call(finish_kernel, grid=(2 * half // block,), out_shape=(jax.S...]
    pallas_call x1, Pallas kernels: 110 us -> 106 us  [main_call(): pl.pallas_call(functools.partial(main_kernel, p, total_rows, scale), out_...]
    unnamed x0 -> x4, local copies, waits for them, and re-layouts: none -> 1.33 us
where the time goes in v3:
time: 110 us
  Pallas kernels  108 us (98%)
  local copies, waits for them, and re-layouts  1.33 us (1%)
    pallas_call x1, Pallas kernels, main_call(): pl.pallas_call(functools.partial(main_kernel, p, total_rows, scale), out_...  106 us

profile of v3, /device:TPU:0, one launch (start us, length us, event | category | flops | bytes accessed | tf_op | source)
XLA Modules:
  0.0 110.1 jit_solution(17296494823168090370)
XLA Ops:
  0.6 0.0 copy-start
  0.6 0.7 copy-done
  1.3 0.0 copy-start.1
  1.3 0.7 copy-done.1
  2.0 106.1 %shard_map.50 = (bf16[2,16,32768]{2,1,0:T(8,128)(2,1)S(1)}, f32[2,8,8]{2,1,0:T(8,128)S(1)}, f32[8,128]{1,0:T(8,128)S(1)}) custom-call(bf16[64,65536]{1,0:T(8,128)(2,1)} %x_ref.1, f32[8,64]{1,0:T(8,128)S(1)} %bitcast.3, s32[1,8]{1,0:T(1,128)S(1)} %copy-done.1), custom_call_target="tpu_custom_call" | custom-call | tf_op jit(solution)/shard_map/pallas_call | solution.py:933
  108.1 1.9 %shard_map.51 = (f32[8,65536]{1,0:T(8,128)}, f32[8,64]{1,0:T(8,128)}) custom-call(bf16[2,16,32768]{2,1,0:T(8,128)(2,1)S(1)} %get-tuple-element.7.pf_ref, f32[2,8,8]{2,1,0:T(8,128)S(1)} %get-tuple-element.8.alpha_ref, f32[8,128]{1,0:T(8,128)S(1)} %get-tuple-element.9.sol_ref), custom_call_target="tpu_custom_call" | custom-call | tf_op jit(solution)/shard_map/pallas_call | solution.py:990
Async XLA Ops:
  0.6 0.7 copy-start
  1.3 0.7 copy-start.1
